TPU v7x, 32 devices: a whole 2x2x4 slice. The times are simulated.
32 devices in a mesh: groups: 2 (over y), view: 4 (over z), head: 2 (over x), dp: 2 (over core).
Axes of the slice: x: 2, y: 2, z: 4, core: 2. Of those that a mesh axis runs over, the one named last changes fastest.
Arguments:
- ray_tokens: bfloat16 [512, 1024], P(('groups', 'view', 'dp')), parts along dimension 0, may hold values from -6 to 6
- up_weight: bfloat16 [1024, 4096], P('dp', 'head'), may hold values from -0.1875 to 0.1875
- down_weight: bfloat16 [1024, 4096], P('dp', 'head'), may hold values from -0.09375 to 0.09375
- key_weight: bfloat16 [1024, 5120], P('dp', 'head'), may hold values from -0.1875 to 0.1875
- value_weight: bfloat16 [1024, 5120], P('dp', 'head'), may hold values from -0.1875 to 0.1875
- video_queries: bfloat16 [2048, 5120], P(('groups', 'view', 'dp'), 'head'), parts along dimension 0, may hold values from -204 to 204
- video_keys: bfloat16 [2048, 5120], P(('groups', 'view', 'dp'), 'head'), parts along dimension 0, may hold values from -6 to 6
- video_values: bfloat16 [2048, 5120], P(('groups', 'view', 'dp'), 'head'), parts along dimension 0, may hold values from -6 to 6
- cross_queries: bfloat16 [2048, 5120], P(('groups', 'view', 'dp'), 'head'), parts along dimension 0, may hold values from -204 to 204
Outputs:
- attended: bfloat16 [2048, 5120], P(('groups', 'view', 'dp'), 'head'), parts along dimension 0
There are 2 independent parts, one for each index of `groups`. A program takes and returns all parts, laid end to end along the dimension named above; an argument that names none is the same for every part. Nothing has to cross between parts.
All inputs are finite; a program needn't handle non-finite values.
Results may differ from a plain program's by a relative error of at most 0.025.
Values may be sent and summed in bfloat16 or wider, within the bound.
No kernel may reach another device: no remote copies, remote signals or barrier semaphores. Data moves between devices by JAX's collectives and lax.ppermute only.
A program may use at most 64 MiB of HBM per device.

v0:
```python
import jax
import jax.numpy as jnp
from jax import lax
from jax.sharding import PartitionSpec as P

HEAD_DIM = 128


epsilon = 1e-06


def rms_normed(values_in):
    widened = values_in.astype(jnp.float32)
    mean_square = jnp.mean(widened * widened, axis=1, keepdims=True)
    return widened * lax.rsqrt(mean_square + epsilon)


def empty_state(head_count, row_count):
    running_max = jnp.full((head_count, row_count), -1e30, jnp.float32)
    running_sum = jnp.zeros((head_count, row_count), jnp.float32)
    weighted = jnp.zeros((head_count, row_count, HEAD_DIM), jnp.float32)
    return (running_max, running_sum, weighted)


def absorb(state_now, query_head_rows, key_piece, value_piece):
    running_max, running_sum, weighted = state_now
    head_count = query_head_rows.shape[1]
    key_head_rows = key_piece.reshape(key_piece.shape[0], head_count, HEAD_DIM)
    value_head_rows = value_piece.reshape(value_piece.shape[0], head_count, HEAD_DIM)
    scores = jnp.einsum(
        "xrz,frz->rxf", query_head_rows, key_head_rows, preferred_element_type=jnp.float32
    ) * HEAD_DIM ** (-0.5)
    new_max = jnp.maximum(running_max, jnp.max(scores, axis=2))
    exponent = jnp.exp(scores - new_max[:, :, None])
    running_sum = jnp.sum(exponent, axis=2)
    weighted = jnp.einsum(
        "bau,uby->bay",
        exponent.astype(jnp.bfloat16),
        value_head_rows,
        preferred_element_type=jnp.float32,
    )
    return (new_max, running_sum, weighted)


def finish(state_now):
    running_max, running_sum, weighted = state_now
    result = weighted / running_sum[:, :, None]
    head_count, row_count = running_sum.shape
    return result.transpose(1, 0, 2).reshape(row_count, head_count * HEAD_DIM)


def body(
    ray_tokens,
    up_weight,
    down_weight,
    key_weight,
    value_weight,
    video_queries,
    video_keys,
    video_values,
    cross_queries,
):
    row_count = video_queries.shape[0]
    head_count = video_queries.shape[1] // HEAD_DIM
    up_full, down_full, key_full, value_full = (
        lax.all_gather(up_weight, "dp", axis=0, tiled=True),
        lax.all_gather(down_weight, "dp", axis=0, tiled=True),
        lax.all_gather(key_weight, "dp", axis=0, tiled=True),
        lax.all_gather(value_weight, "dp", axis=0, tiled=True),
    )
    normed = rms_normed(ray_tokens).astype(jnp.bfloat16)
    hidden = jax.nn.gelu(jnp.dot(normed, up_full, preferred_element_type=jnp.float32)).astype(
        jnp.bfloat16
    )
    partial_branch = lax.dot_general(
        hidden, down_full, (((1,), (1,)), ((), ())), preferred_element_type=jnp.float32
    )
    branch = lax.psum(partial_branch, "head")
    rays = (ray_tokens.astype(jnp.float32) + branch).astype(jnp.bfloat16)
    cross_heads = cross_queries.reshape(row_count, head_count, HEAD_DIM)
    piece = lax.all_gather(rays, ("view", "dp"), axis=0, tiled=True)
    piece_keys = jnp.dot(piece, key_full, preferred_element_type=jnp.float32).astype(jnp.bfloat16)
    piece_values = jnp.dot(piece, value_full, preferred_element_type=jnp.float32).astype(
        jnp.bfloat16
    )
    cross_state = absorb(empty_state(head_count, row_count), cross_heads, piece_keys, piece_values)
    cross = finish(cross_state)
    local_head_group = video_queries.reshape(row_count, head_count, HEAD_DIM)
    own_state = absorb(
        empty_state(head_count, row_count),
        local_head_group,
        lax.all_gather(video_keys, ("view", "dp"), axis=0, tiled=True),
        lax.all_gather(video_values, ("view", "dp"), axis=0, tiled=True),
    )
    own = finish(own_state)
    return (own + cross).astype(jnp.bfloat16)


def solution(mesh):
    in_specs = (
        P(("groups", "view", "dp"), None),
        P("dp", "head"),
        P("dp", "head"),
        P("dp", "head"),
        P("dp", "head"),
        P(("groups", "view", "dp"), "head"),
        P(("groups", "view", "dp"), "head"),
        P(("groups", "view", "dp"), "head"),
        P(("groups", "view", "dp"), "head"),
    )
    out_specs = P(("groups", "view", "dp"), "head")
    return jax.shard_map(body, mesh=mesh, in_specs=in_specs, out_specs=out_specs, check_vma=False)
```

profile of v0, /device:TPU:0, one launch (start us, length us, event | category | flops | bytes accessed | tf_op | source)
XLA Modules:
  0.0 245.0 jit_solution(7052260956452265076)
XLA Ops:
  8.2 17.1 %all-gather.11.cloned.1.call-done = bf16[1024,2048]{1,0:T(8,128)(2,1)} async-done(((bf16[512,2048]{1,0:T(8,128)(2,1)}), bf16[1024,2048]{1,0:T(8,128)(2,1)}) %all-gather.11.cloned.1.call-update) | async-done | bytes 4194320 | tf_op jit(solution)/shard_map/all_gather | solution.py:66
  25.3 16.4 %all-gather.13.cloned.1.call-done = bf16[1024,2048]{1,0:T(8,128)(2,1)} async-done(((bf16[512,2048]{1,0:T(8,128)(2,1)}), bf16[1024,2048]{1,0:T(8,128)(2,1)}) %all-gather.13.cloned.1.call-update) | async-done | bytes 4194320 | tf_op jit(solution)/shard_map/all_gather | solution.py:67
  41.7 6.2 %fusion.29 = f32[32,1024]{1,0:T(8,128)} fusion(bf16[1024,2048]{1,0:T(8,128)(2,1)} %all-gather.13.cloned.1.call-done, bf16[1024,2048]{1,0:T(8,128)(2,1)} %all-gather.11.cloned.1.call-done, bf16[32,1024]{1,0:T(8,128)(2,1)S(1)} %copy-done.5, f32[32]{0:T(128)S(1)} %add_rsqrt_fusion), kind=kOutput, calls=%fused_computation.36 | convolution fusion | flops 269123584 | bytes 8585344 | tf_op jit(solution)/shard_map/dot_general | solution.py:75
  49.2 1.1 copy.18
  51.1 1.1 copy.23
  52.5 18.3 %all-reduce.2.cloned.1.call-done = f32[32,1024]{1,0:T(8,128)} async-done(((f32[32,1024]{1,0:T(8,128)}), f32[32,1024]{1,0:T(8,128)}) %all-reduce.2.cloned.1.call-update) | async-done | bytes 131088 | tf_op jit(solution)/shard_map/psum | solution.py:78
  70.8 0.9 fusion.28
  71.7 14.9 %all_gather.25 = bf16[256,1024]{1,0:T(8,128)(2,1)S(1)} all-gather(bf16[32,1024]{1,0:T(8,128)(2,1)S(1)} %fusion.28), channel_id=1, replica_groups=mesh['groups'=2,'view'=4,'head'=2,'dp'=2] {'view','dp'}, dimensions={0}, use_global_device_ids=true | all-gather | bytes 589824 | tf_op jit(solution)/shard_map/all_gather | solution.py:81
  86.6 0.9 all-gather.15.cloned.1.call-done
  87.6 4.0 %convolution_convert_fusion.1 = bf16[256,2560]{1,0:T(8,128)(2,1)S(1)} fusion(bf16[256,1024]{1,0:T(8,128)(2,1)S(1)} %all_gather.25, bf16[1024,2560]{1,0:T(8,128)(2,1)} %all-gather.15.cloned.1.call-done), kind=kOutput, calls=%fused_computation.8 | convolution fusion | flops 1342832640 | bytes 7077888 | tf_op jit(solution)/shard_map/dot_general | solution.py:82
  91.6 1.4 copy.22
  93.0 12.3 %all-gather.17.cloned.1.call-done = bf16[1024,2560]{1,0:T(8,128)(2,1)} async-done(((bf16[512,2560]{1,0:T(8,128)(2,1)}), bf16[1024,2560]{1,0:T(8,128)(2,1)}) %all-gather.17.cloned.1.call-update) | async-done | bytes 5242896 | tf_op jit(solution)/shard_map/all_gather | solution.py:69
  105.4 4.0 %convolution_convert_fusion = bf16[256,2560]{1,0:T(8,128)(2,1)S(1)} fusion(bf16[256,1024]{1,0:T(8,128)(2,1)S(1)} %all_gather.25, bf16[1024,2560]{1,0:T(8,128)(2,1)} %all-gather.17.cloned.1.call-done), kind=kOutput, calls=%fused_computation.7 | convolution fusion | flops 1342832640 | bytes 7077888 | tf_op jit(solution)/shard_map/dot_general | solution.py:83
  109.4 1.5 copy.26
  110.8 2.1 bitcast_reduce_fusion
  113.4 51.1 %all-gather.7.cloned.1.call-done = bf16[1024,2560]{0,1:T(8,128)(2,1)} async-done(((bf16[128,2560]{0,1:T(8,128)(2,1)}), bf16[1024,2560]{0,1:T(8,128)(2,1)}) %all-gather.7.cloned.1.call-update) | async-done | bytes 5242896 | tf_op jit(solution)/shard_map/all_gather | solution.py:92
  164.5 4.2 %multiply_reduce_fusion = (f32[20,128]{1,0:T(8,128)S(1)}, f32[20,128,1024]{2,1,0:T(8,128)S(1)}) fusion(bf16[128,20,128]{0,2,1:T(8,128)(2,1)S(1)} %bitcast.44, bf16[1024,20,128]{0,2,1:T(8,128)(2,1)} %bitcast.42), kind=kOutput, calls=%fused_computation.1 | convolution fusion | flops 676328960 | bytes 16394240 | tf_op jit(solution)/shard_map/xrz,frz->rxf/dot_general | solution.py:30
  168.7 4.2 %copy-done = f32[20,128,1024]{2,1,0:T(8,128)} copy-done((f32[20,128,1024]{2,1,0:T(8,128)}, f32[20,128,1024]{2,1,0:T(8,128)S(1)}, u32[]{:S(2)}) %copy-start) | copy-done | bytes 10485784
  172.9 2.1 fusion
  175.0 45.3 %all-gather.9.cloned.1.call-done = bf16[1024,2560]{1,0:T(8,128)(2,1)} async-done(((bf16[128,2560]{1,0:T(8,128)(2,1)}), bf16[1024,2560]{1,0:T(8,128)(2,1)}) %all-gather.9.cloned.1.call-update) | async-done | bytes 5242896 | tf_op jit(solution)/shard_map/all_gather | solution.py:93
  220.3 7.9 %copy.21 = bf16[1024,2560]{0,1:T(8,128)(2,1)} copy(bf16[1024,2560]{1,0:T(8,128)(2,1)} %all-gather.9.cloned.1.call-done) | data formatting | bytes 10485760 | tf_op jit(solution)/shard_map/all_gather | solution.py:93
  228.3 7.9 %fusion.9 = f32[128,20,128]{0,2,1:T(8,128)S(1)} fusion(bf16[1024,20,128]{0,2,1:T(8,128)(2,1)} %bitcast.41, f32[20,128,1024]{2,1,0:T(8,128)} %copy-done, f32[20,128]{1,0:T(8,128)S(1)} %broadcast_maximum_fusion.1), kind=kOutput, calls=%fused_computation.14 | convolution fusion | flops 678952960 | bytes 17049600 | tf_op jit(solution)/shard_map/bau,uby->bay/dot_general | solution.py:36
  236.2 0.8 fusion.14
  237.0 1.1 copy.28
  (31 shorter events, 4.4 us)
Async XLA Ops:
  6.5 1.5 copy-start.5
  6.5 18.8 %all-gather.11.cloned.1.call-start = ((), (), s32[]{:S(2)}) async-start(), calls=%async_computation.2 | async-start | bytes 6291456 | tf_op jit(solution)/shard_map/all_gather | solution.py:66
  7.3 34.5 %all-gather.13.cloned.1.call-start = ((), (), s32[]{:S(2)}) async-start(), calls=%async_computation.3 | async-start | bytes 6291456 | tf_op jit(solution)/shard_map/all_gather | solution.py:67
  8.0 62.8 %all-reduce.2.cloned.1.call-start = ((), (), s32[]{:S(2)}) async-start(), calls=%async_computation.4 | async-start | bytes 262144 | tf_op jit(solution)/shard_map/psum | solution.py:78
  48.0 1.3 copy-start.2
  48.0 39.6 %all-gather.15.cloned.1.call-start = ((), (), s32[]{:S(2)}) async-start(), calls=%async_computation.5 | async-start | bytes 7864320 | tf_op jit(solution)/shard_map/all_gather | solution.py:68
  48.5 2.5 %copy-start.3 = (bf16[128,2560]{1,0:T(8,128)(2,1)S(1)}, bf16[128,2560]{1,0:T(8,128)(2,1)}, u32[]{:S(2)}) copy-start(bf16[128,2560]{1,0:T(8,128)(2,1)} %param.17) | copy-start | bytes 1966084
  48.6 56.8 %all-gather.17.cloned.1.call-start = ((), (), s32[]{:S(2)}) async-start(), calls=%async_computation.6 | async-start | bytes 7864320 | tf_op jit(solution)/shard_map/all_gather | solution.py:69
  49.1 3.0 %copy-start.4 = (bf16[128,2560]{1,0:T(8,128)(2,1)S(1)}, bf16[128,2560]{1,0:T(8,128)(2,1)}, u32[]{:S(2)}) copy-start(bf16[128,2560]{1,0:T(8,128)(2,1)} %param.14) | copy-start | bytes 1966084
  49.2 115.3 %all-gather.7.cloned.1.call-start = ((), (), s32[]{:S(2)}) async-start(), calls=%async_computation | async-start | bytes 5898240 | tf_op jit(solution)/shard_map/all_gather | solution.py:92
  50.3 170.0 %all-gather.9.cloned.1.call-start = ((), (), s32[]{:S(2)}) async-start(), calls=%async_computation.1 | async-start | bytes 5898240 | tf_op jit(solution)/shard_map/all_gather | solution.py:93
  168.7 4.2 %copy-start = (f32[20,128,1024]{2,1,0:T(8,128)}, f32[20,128,1024]{2,1,0:T(8,128)S(1)}, u32[]{:S(2)}) copy-start(f32[20,128,1024]{2,1,0:T(8,128)S(1)} %get-tuple-element.8) | copy-start | bytes 31457284
  228.3 7.9 %copy-start.1 = (bf16[256,2560]{0,1:T(8,128)(2,1)S(1)}, bf16[256,2560]{0,1:T(8,128)(2,1)}, u32[]{:S(2)}) copy-start(bf16[256,2560]{0,1:T(8,128)(2,1)} %copy.26) | copy-start | bytes 3932164
Sparse Core Ops, SparseCore 0:
  8.9 16.3 all-gather.10
  26.8 14.8 all-gather.12
  48.1 22.6 all-reduce.1
  72.2 15.2 all-gather.14
  88.9 16.3 all-gather.16
  106.8 57.6 all-gather.6
  166.1 54.1 all-gather.8
where the time goes:
time: 245 us
  waiting for transfers between devices  165 us (67%)
  matrix products  29.2 us (12%)
  local copies, waits for them, and re-layouts  18.6 us (8%)
  blocking collectives  14.9 us (6%)
  between operations  13.6 us (6%)
  other arithmetic  3.62 us (1%)
    all_gather x1, waiting for transfers between devices, body(): lax.all_gather(video_keys, ('view', 'dp'), axis=0, tiled=True)  51.1 us
    all_gather x1, waiting for transfers between devices, body(): lax.all_gather(video_values, ('view', 'dp'), axis=0, tiled=True)  45.3 us
    psum x1, waiting for transfers between devices, body(): branch = lax.psum(partial_branch, 'head')  18.3 us
    all_gather x1, waiting for transfers between devices, body(): lax.all_gather(up_weight, 'dp', axis=0, tiled=True)  17.1 us
    all_gather x1, waiting for transfers between devices, body(): lax.all_gather(down_weight, 'dp', axis=0, tiled=True)  16.4 us
    all_gather x1, blocking collectives, body(): piece = lax.all_gather(rays, ('view', 'dp'), axis=0, tiled=True)  14.9 us
    all_gather x1, waiting for transfers between devices, body(): lax.all_gather(value_weight, 'dp', axis=0, tiled=True)  12.3 us
    dot_general x2, matrix products, absorb(): jnp.einsum('bau,uby->bay', exponent.astype(jnp.bfloat16), value_head_rows...  8.71 us
  transfers between devices with their start and end apart: 7, of which 7 were waited for; matrix products, arithmetic and copies ran while one was open for 9% of the time, Pallas kernels for 0%

commit v1 on v0

--- a/solution.py
+++ b/solution.py
@@ -1,9 +1,15 @@
+import functools
+import math
+
 import jax
 import jax.numpy as jnp
 from jax import lax
+from jax.experimental import pallas as pl
+from jax.experimental.pallas import tpu as pltpu
 from jax.sharding import PartitionSpec as P
 
 HEAD_DIM = 128
+EXPONENT = HEAD_DIM ** (-0.5) * math.log2(math.e)
 
 
 epsilon = 1e-06
@@ -43,13 +49,13 @@
 
 
 def finish(state_now):
-    running_max, running_sum, weighted = state_now
+    _, running_sum, weighted = state_now
     result = weighted / running_sum[:, :, None]
     head_count, row_count = running_sum.shape
     return result.transpose(1, 0, 2).reshape(row_count, head_count * HEAD_DIM)
 
 
-def body(
+def gathered_body(
     ray_tokens,
     up_weight,
     down_weight,
@@ -96,17 +102,326 @@
     return (own + cross).astype(jnp.bfloat16)
 
 
+VMEM = pl.BlockSpec(memory_space=pltpu.VMEM)
+HBM = pl.BlockSpec(memory_space=pltpu.HBM)
+SMEM = pl.BlockSpec(memory_space=pltpu.SMEM)
+MIB = 2**20
+
+
+def local_call(
+    kernel, megabytes, flops, transcendentals, out_shape, scalars, *arrays, streamed=(), scratch=()
+):
+    moved = sum(array.size * array.dtype.itemsize for array in arrays + tuple(streamed))
+    call = pl.pallas_call(
+        kernel,
+        in_specs=[SMEM] * len(scalars) + [VMEM] * len(arrays) + [HBM] * len(streamed),
+        scratch_shapes=list(scratch),
+        out_specs=jax.tree.map(lambda _: VMEM, out_shape),
+        out_shape=out_shape,
+        cost_estimate=pl.CostEstimate(
+            flops=flops, transcendentals=transcendentals, bytes_accessed=moved
+        ),
+        compiler_params=pltpu.CompilerParams(vmem_limit_bytes=megabytes * MIB),
+    )
+    scalars = (scalar.astype(jnp.int32).reshape(1) for scalar in scalars)
+    streamed = (pltpu.with_memory_space_constraint(array, pltpu.HBM) for array in streamed)
+    return call(*scalars, *arrays, *streamed)
+
+
+def matmul(left, right):
+    return jnp.dot(left, right, preferred_element_type=jnp.float32)
+
+
+def matmul_t(left, right):
+    return lax.dot_general(
+        left, right, (((1,), (1,)), ((), ())), preferred_element_type=jnp.float32
+    )
+
+
+def attend(query, keys, values):
+    scores = matmul_t(query, keys)
+    largest = jnp.max(scores, axis=1, keepdims=True)
+    weights = jnp.exp2((scores - largest) * EXPONENT)
+    total = jnp.sum(weights, axis=1, keepdims=True)
+    return matmul(weights.astype(jnp.bfloat16), values) / total
+
+
+def head_columns(head):
+    return pl.ds(pl.multiple_of(head * HEAD_DIM, HEAD_DIM), HEAD_DIM)
+
+
+def pack_kernel(views, offset, view, *refs):
+    sources, results, arrived = refs[:3], refs[3:-1], refs[-1]
+    span = sources[0].shape[1] // views
+    copies = []
+    for step, result in enumerate(results):
+        start = pl.multiple_of((view[0] ^ step) * span + offset, HEAD_DIM)
+        for slot, source in enumerate(sources):
+            copies.append(
+                pltpu.make_async_copy(
+                    source.at[:, pl.ds(start, result.shape[2])],
+                    result.at[slot],
+                    arrived.at[step, slot],
+                )
+            )
+    for copy in copies:
+        copy.start()
+    for copy in copies:
+        copy.wait()
+
+
+def pack(view, views, offset, width, keys, values, queries):
+    rows = keys.shape[0]
+    return local_call(
+        functools.partial(pack_kernel, views, offset),
+        8,
+        keys.size,
+        0,
+        [jax.ShapeDtypeStruct((3, rows, width), jnp.bfloat16)] * views,
+        (view,),
+        streamed=(keys, values, queries),
+        scratch=(pltpu.SemaphoreType.DMA((views, 3)),),
+    )
+
+
+def ray_kernel(aligned, here_ref, there_ref, *refs):
+    sources, (keep, send), held, arrived = refs[:4], refs[4:6], refs[6:10], refs[10]
+    copies = [
+        pltpu.make_async_copy(source, target, arrived.at[index])
+        for index, (source, target) in enumerate(zip(sources, held))
+    ]
+    for copy in copies:
+        copy.start()
+    same = aligned[0] == 1
+    here, there = here_ref[...].astype(jnp.float32), there_ref[...].astype(jnp.float32)
+    square = jnp.sum(here * here + there * there, axis=1, keepdims=True)
+    factor = lax.rsqrt(square / (2 * here.shape[1]) + epsilon)
+    here = (here * factor).astype(jnp.bfloat16)
+    there = (there * factor).astype(jnp.bfloat16)
+    near, far = jnp.where(same, here, there), jnp.where(same, there, here)
+    copies[0].wait()
+    copies[1].wait()
+    hidden = jax.nn.gelu(matmul(near, held[0][...]) + matmul(far, held[1][...]))
+    hidden = hidden.astype(jnp.bfloat16)
+    copies[2].wait()
+    branch_near = matmul_t(hidden, held[2][...])
+    copies[3].wait()
+    branch_far = matmul_t(hidden, held[3][...])
+    keep[...] = jnp.where(same, branch_near, branch_far) + here_ref[...].astype(jnp.float32)
+    send[...] = jnp.where(same, branch_far, branch_near)
+
+
+def ray_layer(aligned, here, there, weights):
+    return local_call(
+        ray_kernel,
+        20,
+        8 * here.size * weights[0].shape[1],
+        0,
+        [jax.ShapeDtypeStruct(here.shape, jnp.float32)] * 2,
+        (aligned,),
+        here,
+        there,
+        streamed=weights,
+        scratch=[pltpu.VMEM(weight.shape, weight.dtype) for weight in weights]
+        + [pltpu.SemaphoreType.DMA((4,))],
+    )
+
+
+def own_kernel(views, *refs):
+    pieces, others, results = refs[:views], refs[views : 2 * views], refs[2 * views :]
+
+    @pl.loop(0, results[0].shape[1] // HEAD_DIM)
+    def _(head):
+        columns = head_columns(head)
+        keys = jnp.concatenate([piece[0, :, columns] for piece in pieces + others], axis=0)
+        values = jnp.concatenate([piece[1, :, columns] for piece in pieces + others], axis=0)
+        for piece, result in zip(pieces, results):
+            result[:, columns] = attend(piece[2, :, columns], keys, values).astype(jnp.bfloat16)
+
+
+def own_attention(pieces, others):
+    views = len(pieces)
+    _, rows, width = pieces[0].shape
+    area = 2 * views * views * rows * rows * (width // HEAD_DIM)
+    out_shape = [jax.ShapeDtypeStruct((rows, width), jnp.bfloat16)] * views
+    kernel = functools.partial(own_kernel, views)
+    return local_call(kernel, 12, 4 * area * HEAD_DIM, area, out_shape, (), *pieces, *others)
+
+
+def cross_kernel(
+    heads,
+    aligned,
+    here,
+    there,
+    peer_here,
+    peer_there,
+    key_near,
+    key_far,
+    value_near,
+    value_far,
+    query,
+    result,
+):
+    same = aligned[0] == 1
+    first = jnp.concatenate([here[...], peer_here[...]], axis=0)
+    second = jnp.concatenate([there[...], peer_there[...]], axis=0)
+    near, far = jnp.where(same, first, second), jnp.where(same, second, first)
+    step = heads * HEAD_DIM
+
+    @pl.loop(0, query.shape[1] // step)
+    def _(group):
+        block = pl.ds(pl.multiple_of(group * step, step), step)
+        keys = (matmul(near, key_near[:, block]) + matmul(far, key_far[:, block])).astype(
+            jnp.bfloat16
+        )
+        values = (matmul(near, value_near[:, block]) + matmul(far, value_far[:, block])).astype(
+            jnp.bfloat16
+        )
+        for head in range(heads):
+            inner = slice(head * HEAD_DIM, (head + 1) * HEAD_DIM)
+            outer = head_columns(group * heads + head)
+            result[:, outer] = attend(query[:, outer], keys[:, inner], values[:, inner])
+
+
+def cross_attention(aligned, rays, weights, queries):
+    rows, width = queries.shape
+    ray_rows, depth = 2 * rays[0].shape[0], rays[0].shape[1]
+    count = width // HEAD_DIM
+    heads = max(group for group in range(1, 11) if count % group == 0)
+    return local_call(
+        functools.partial(cross_kernel, heads),
+        20,
+        8 * ray_rows * depth * width + 4 * rows * ray_rows * width,
+        rows * ray_rows * count,
+        jax.ShapeDtypeStruct((rows, width), jnp.float32),
+        (aligned,),
+        *rays,
+        *weights,
+        queries,
+    )
+
+
+def join_kernel(views, offsets, view, cross, *refs):
+    pieces, result = refs[:-1], refs[-1]
+    span = cross.shape[1] // views
+    for index, piece in enumerate(pieces):
+        chunk, step = divmod(index, views)
+        start = pl.multiple_of((view[0] ^ step) * span + offsets[chunk], HEAD_DIM)
+        columns = pl.ds(start, piece.shape[1])
+        result[:, columns] = (cross[:, columns] + piece[...].astype(jnp.float32)).astype(
+            jnp.bfloat16
+        )
+
+
+def join(view, cross, chunks, offsets):
+    pieces = [piece for chunk in chunks for piece in chunk]
+    kernel = functools.partial(join_kernel, len(chunks[0]), offsets)
+    out_shape = jax.ShapeDtypeStruct(cross.shape, jnp.bfloat16)
+    return local_call(kernel, 6, 2 * cross.size, 0, out_shape, (view,), cross, *pieces)
+
+
+def swapped(values, axis):
+    return lax.ppermute(values, axis, [(0, 1), (1, 0)])
+
+
+def exchanged(values, views, step):
+    return lax.ppermute(values, "view", [(i, i ^ step) for i in range(views)])
+
+
+def exchanged_body(views, *arrays):
+    return exchange_heads(views, *arrays)
+
+
+def exchange_heads(
+    views,
+    ray_tokens,
+    up_weight,
+    down_weight,
+    key_weight,
+    value_weight,
+    video_queries,
+    video_keys,
+    video_values,
+    cross_queries,
+):
+    view, side, core = (lax.axis_index(axis) for axis in ("view", "head", "dp"))
+    span = video_queries.shape[1] // views
+    widths, offsets = chunk_columns(span)
+    aligned = side == core
+
+    half = ray_tokens.shape[1] // 2
+    ray_half = lax.dynamic_slice(ray_tokens, (0, side * half), (ray_tokens.shape[0], half))
+    ray_rows = jnp.concatenate(
+        [ray_half]
+        + [exchanged(ray_half, views, step) for step in range(1, views)],
+        axis=0,
+    )
+    up_peer = swapped(up_weight, "dp")
+    down_peer = swapped(down_weight, "dp")
+    key_peer = swapped(key_weight, "dp")
+    value_peer = swapped(value_weight, "dp")
+
+    packed = [
+        pack(view, views, *columns, video_keys, video_values, video_queries)
+        for columns in zip(offsets, widths)
+    ]
+    chunks = [
+        [exchanged(piece, views, step) if step else piece for step, piece in enumerate(pieces)]
+        for pieces in packed
+    ]
+
+    other_half = swapped(ray_rows, "head")
+    keep, send = ray_layer(
+        aligned, ray_rows, other_half, (up_weight, up_peer, down_weight, down_peer)
+    )
+    here = (keep + swapped(send, "head")).astype(jnp.bfloat16)
+    there = swapped(here, "head")
+    rays = (here, there, swapped(here, "dp"), swapped(there, "dp"))
+    cross = cross_attention(
+        aligned, rays, (key_weight, key_peer, value_weight, value_peer), cross_queries
+    )
+
+    returned = []
+    for pieces in chunks:
+        others = [swapped(piece, "dp") for piece in pieces]
+        results = own_attention(pieces, others)
+        returned.append(
+            [exchanged(part, views, step) if step else part for step, part in enumerate(results)]
+        )
+    return join(view, cross, returned, offsets)
+
+
+def chunk_columns(span):
+    heads = span // HEAD_DIM
+    first = (heads + 1) // 2
+    widths = [count * HEAD_DIM for count in (first, heads - first) if count]
+    return widths, [sum(widths[:index]) for index in range(len(widths))]
+
+
 def solution(mesh):
-    in_specs = (
-        P(("groups", "view", "dp"), None),
-        P("dp", "head"),
-        P("dp", "head"),
-        P("dp", "head"),
-        P("dp", "head"),
-        P(("groups", "view", "dp"), "head"),
-        P(("groups", "view", "dp"), "head"),
-        P(("groups", "view", "dp"), "head"),
-        P(("groups", "view", "dp"), "head"),
-    )
-    out_specs = P(("groups", "view", "dp"), "head")
-    return jax.shard_map(body, mesh=mesh, in_specs=in_specs, out_specs=out_specs, check_vma=False)
+    row_axes = ("groups", "view", "dp")
+    in_specs = (P(row_axes, None),) + (P("dp", "head"),) * 4 + (P(row_axes, "head"),) * 4
+    out_specs = P(row_axes, "head")
+
+    views = mesh.shape["view"]
+
+    def mapped(body):
+        return jax.shard_map(
+            body, mesh=mesh, in_specs=in_specs, out_specs=out_specs, check_vma=False
+        )
+
+    def whole(*arrays):
+        span = arrays[5].shape[1] // mesh.shape["head"] // views
+        exchange = (
+            mesh.shape["dp"] == 2
+            and mesh.shape["head"] == 2
+            and views > 1
+            and views & (views - 1) == 0
+            and span % HEAD_DIM == 0
+        )
+        if not exchange:
+            return mapped(gathered_body)(*arrays)
+        step = mapped(functools.partial(exchanged_body, views))
+        return step(*arrays)
+
+    return whole

time: 245 us -> 126 us (0.51)
  waiting for transfers between devices: 165 us -> 62.5 us
  starting transfers between devices: 0.24 us -> 36 us
  matrix products: 29.2 us -> 0 us
  Pallas kernels: 0 us -> 25.2 us
  local copies, waits for them, and re-layouts: 18.6 us -> 1.69 us
  blocking collectives: 14.9 us -> 0 us
  between operations: 13.6 us -> 0.25 us
  other arithmetic: 3.62 us -> 0.05 us
    all_gather x6 -> x0, waiting for transfers between devices: 143 us -> none  [the longest x1 51.1 us: body(): lax.all_gather(video_keys, ('view', 'dp'), axis=0, tiled=True)]
    ppermute x0 -> x32, waiting for transfers between devices: none -> 62.5 us  [the longest x15 51.2 us: exchanged(): return lax.ppermute(values, 'view', [(i, i ^ step) for i in range(views)])]
    ppermute x0 -> x32, starting transfers between devices: none -> 36 us  [the longest x15 29.2 us: exchanged(): return lax.ppermute(values, 'view', [(i, i ^ step) for i in range(views)])]
    dot_general x7 -> x0, matrix products: 29.2 us -> none  [the longest x2 8.71 us: absorb(): jnp.einsum('bau,uby->bay', exponent.astype(jnp.bfloat16), value_head_rows...]
    pallas_call x0 -> x7, Pallas kernels: none -> 25.2 us  [local_call(): return call(*scalars, *arrays, *streamed)]
    psum x1 -> x0, waiting for transfers between devices: 18.3 us -> none  [body(): branch = lax.psum(partial_branch, 'head')]
    all_gather x1 -> x0, blocking collectives: 14.9 us -> none  [body(): piece = lax.all_gather(rays, ('view', 'dp'), axis=0, tiled=True)]
    all_gather x1 -> x0, local copies, waits for them, and re-layouts: 7.95 us -> none  [body(): lax.all_gather(video_values, ('view', 'dp'), axis=0, tiled=True)]
  transfers between devices with their start and end apart: 7 -> 32, of which waited for: 7 -> 14; matrix products, arithmetic and copies ran while one was open for 9% -> 0% of each run, Pallas kernels for 0% -> 19%
where the time goes in v1:
time: 126 us
  waiting for transfers between devices  62.5 us (50%)
  starting transfers between devices  36 us (29%)
  Pallas kernels  25.2 us (20%)
  local copies, waits for them, and re-layouts  1.69 us (1%)
    ppermute x15, waiting for transfers between devices, exchanged(): return lax.ppermute(values, 'view', [(i, i ^ step) for i in range(views)])  51.2 us
    ppermute x15, starting transfers between devices, exchanged(): return lax.ppermute(values, 'view', [(i, i ^ step) for i in range(views)])  29.2 us
    pallas_call x7, Pallas kernels, local_call(): return call(*scalars, *arrays, *streamed)  25.2 us
    ppermute x17, waiting for transfers between devices, swapped(): return lax.ppermute(values, axis, [(0, 1), (1, 0)])  11.3 us
    ppermute x17, starting transfers between devices, swapped(): return lax.ppermute(values, axis, [(0, 1), (1, 0)])  6.84 us
  transfers between devices with their start and end apart: 32, of which 14 were waited for; matrix products, arithmetic and copies ran while one was open for 0% of the time, Pallas kernels for 19%

profile of v1, /device:TPU:0, one launch (start us, length us, event | category | flops | bytes accessed | tf_op | source)
XLA Modules:
  0.0 125.8 jit_solution(11926723647288176186)
XLA Ops:
  0.8 3.1 %collective-permute-start = (bf16[32,512]{1,0:T(8,128)(2,1)S(1)}, bf16[32,512]{1,0:T(8,128)(2,1)S(1)}, u32[]{:S(2)}, u32[]{:S(2)}) collective-permute-start(bf16[32,512]{1,0:T(8,128)(2,1)S(1)} %constant_dynamic-slice_fusion), channel_id=1, source_target_pairs={{0,4},{4,0},{8,12},{12,8},{1,5},{5,1},{9,13},{13,9},{2,6},{6,2},{1... | collective-permute-start | bytes 98312 | tf_op jit(solution)/shard_map/ppermute | solution.py:328
  3.9 2.6 %collective-permute-start.1 = (bf16[32,512]{1,0:T(8,128)(2,1)S(1)}, bf16[32,512]{1,0:T(8,128)(2,1)S(1)}, u32[]{:S(2)}, u32[]{:S(2)}) collective-permute-start(bf16[32,512]{1,0:T(8,128)(2,1)S(1)} %constant_dynamic-slice_fusion), channel_id=1, source_target_pairs={{0,8},{4,12},{8,0},{12,4},{1,9},{5,13},{9,1},{13,5},{2,10},{6,14},... | collective-permute-start | bytes 98312 | tf_op jit(solution)/shard_map/ppermute | solution.py:328
  6.5 2.8 %collective-permute-done.1 = bf16[32,512]{1,0:T(8,128)(2,1)S(1)} collective-permute-done((bf16[32,512]{1,0:T(8,128)(2,1)S(1)}, bf16[32,512]{1,0:T(8,128)(2,1)S(1)}, u32[]{:S(2)}, u32[]{:S(2)}) %collective-permute-start.1) | collective-permute-done | bytes 32800 | tf_op jit(solution)/shard_map/ppermute | solution.py:328
  9.3 2.9 %collective-permute-done.2 = bf16[32,512]{1,0:T(8,128)(2,1)S(1)} collective-permute-done((bf16[32,512]{1,0:T(8,128)(2,1)S(1)}, bf16[32,512]{1,0:T(8,128)(2,1)S(1)}, u32[]{:S(2)}, u32[]{:S(2)}) %collective-permute-start.2) | collective-permute-done | bytes 32800 | tf_op jit(solution)/shard_map/ppermute | solution.py:328
  15.1 2.2 %collective-permute-done.3.there_ref = bf16[128,512]{1,0:T(8,128)(2,1)S(1)} collective-permute-done((bf16[128,512]{1,0:T(8,128)(2,1)S(1)}, bf16[128,512]{1,0:T(8,128)(2,1)S(1)}, u32[]{:S(2)}, u32[]{:S(2)}) %collective-permute-start.3) | collective-permute-done | bytes 131104 | tf_op jit(solution)/shard_map/ppermute | solution.py:324
  17.2 5.8 %collective-permute-done.22.refs_1_ = bf16[3,128,256]{2,1,0:T(8,128)(2,1)} collective-permute-done((bf16[3,128,256]{2,1,0:T(8,128)(2,1)S(1)}, bf16[3,128,256]{2,1,0:T(8,128)(2,1)}, u32[]{:S(2)}, u32[]{:S(2)}) %collective-permute-start.22) | collective-permute-done | bytes 196640 | tf_op jit(solution)/shard_map/ppermute | solution.py:328
  24.4 8.6 %collective-permute-done.23.refs_2_ = bf16[3,128,256]{2,1,0:T(8,128)(2,1)S(1)} collective-permute-done((bf16[3,128,256]{2,1,0:T(8,128)(2,1)S(1)}, bf16[3,128,256]{2,1,0:T(8,128)(2,1)S(1)}, u32[]{:S(2)}, u32[]{:S(2)}) %collective-permute-start.23) | collective-permute-done | bytes 196640 | tf_op jit(solution)/shard_map/ppermute | solution.py:328
  33.0 3.9 %collective-permute-start.24 = (bf16[3,128,256]{2,1,0:T(8,128)(2,1)S(1)}, bf16[3,128,256]{2,1,0:T(8,128)(2,1)S(1)}, u32[]{:S(2)}, u32[]{:S(2)}) collective-permute-start(bf16[3,128,256]{2,1,0:T(8,128)(2,1)S(1)} %get-tuple-element.36), channel_id=1, source_target_pairs={{0,12},{4,8},{8,4},{12,0},{1,13},{5,9},{9,5},{13,1},{2,14},{6,10},... | collective-permute-start | bytes 589832 | tf_op jit(solution)/shard_map/ppermute | solution.py:328
  36.9 3.6 %collective-permute-done.24.refs_3_ = bf16[3,128,256]{2,1,0:T(8,128)(2,1)S(1)} collective-permute-done((bf16[3,128,256]{2,1,0:T(8,128)(2,1)S(1)}, bf16[3,128,256]{2,1,0:T(8,128)(2,1)S(1)}, u32[]{:S(2)}, u32[]{:S(2)}) %collective-permute-start.24) | collective-permute-done | bytes 196640 | tf_op jit(solution)/shard_map/ppermute | solution.py:328
  41.2 2.2 %shard_map.93 = (bf16[3,128,384]{2,1,0:T(8,128)(2,1)S(1)}, bf16[3,128,384]{2,1,0:T(8,128)(2,1)S(1)}, bf16[3,128,384]{2,1,0:T(8,128)(2,1)S(1)}, bf16[3,128,384]{2,1,0:T(8,128)(2,1)}) custom-call(s32[1]{0:T(128)} %bitcast.view, bf16[128,2560]{1,0:T(8,128)(2,1)} %refs_0_.5, bf16[128,2560]{1,0:T(8,128)(2,1)} %refs_1_.3, bf16[128,2560]{1,0:T(8,128)(2,1)} %refs_2_.5), custom_call_target="tpu_custom_call" | custom-call | flops 327680 | bytes 1966080 | tf_op jit(solution)/shard_map/pallas_call | solution.py:128
  44.1 9.4 %collective-permute-done.12.refs_1_ = bf16[3,128,384]{2,1,0:T(8,128)(2,1)S(1)} collective-permute-done((bf16[3,128,384]{2,1,0:T(8,128)(2,1)S(1)}, bf16[3,128,384]{2,1,0:T(8,128)(2,1)S(1)}, u32[]{:S(2)}, u32[]{:S(2)}) %collective-permute-start.12) | collective-permute-done | bytes 294944 | tf_op jit(solution)/shard_map/ppermute | solution.py:328
  53.5 2.6 %collective-permute-start.13 = (bf16[3,128,384]{2,1,0:T(8,128)(2,1)S(1)}, bf16[3,128,384]{2,1,0:T(8,128)(2,1)S(1)}, u32[]{:S(2)}, u32[]{:S(2)}) collective-permute-start(bf16[3,128,384]{2,1,0:T(8,128)(2,1)S(1)} %get-tuple-element.27), channel_id=1, source_target_pairs={{0,8},{4,12},{8,0},{12,4},{1,9},{5,13},{9,1},{13,5},{2,10},{6,14},... | collective-permute-start | bytes 884744 | tf_op jit(solution)/shard_map/ppermute | solution.py:328
  56.1 13.4 %collective-permute-done.13.refs_2_ = bf16[3,128,384]{2,1,0:T(8,128)(2,1)S(1)} collective-permute-done((bf16[3,128,384]{2,1,0:T(8,128)(2,1)S(1)}, bf16[3,128,384]{2,1,0:T(8,128)(2,1)S(1)}, u32[]{:S(2)}, u32[]{:S(2)}) %collective-permute-start.13) | collective-permute-done | bytes 294944 | tf_op jit(solution)/shard_map/ppermute | solution.py:328
  69.5 3.5 %collective-permute-start.14 = (bf16[3,128,384]{2,1,0:T(8,128)(2,1)}, bf16[3,128,384]{2,1,0:T(8,128)(2,1)}, u32[]{:S(2)}, u32[]{:S(2)}) collective-permute-start(bf16[3,128,384]{2,1,0:T(8,128)(2,1)} %get-tuple-element.28), channel_id=1, source_target_pairs={{0,12},{4,8},{8,4},{12,0},{1,13},{5,9},{9,5},{13,1},{2,14},{6,10},... | collective-permute-start | bytes 884744 | tf_op jit(solution)/shard_map/ppermute | solution.py:328
  73.7 4.9 %shard_map.91 = (f32[128,512]{1,0:T(8,128)S(1)}, f32[128,512]{1,0:T(8,128)S(1)}) custom-call(s32[1]{0:T(128)} %bitcast.1.aligned, bf16[128,512]{1,0:T(8,128)(2,1)S(1)} %pad_maximum_fusion.here_ref, bf16[128,512]{1,0:T(8,128)(2,1)S(1)} %collective-permute-done.3.there_ref, bf16[512,2048]{1,0:T(8,128)(2,1)} %refs_0_.3, ...), custom_call_target="tpu_custom_call" | custom-call | flops 1073741824 | bytes 8650752 | tf_op jit(solution)/shard_map/pallas_call | solution.py:128
  84.2 3.9 %collective-permute-done.6 = f32[128,512]{1,0:T(8,128)S(1)} collective-permute-done((f32[128,512]{1,0:T(8,128)S(1)}, f32[128,512]{1,0:T(8,128)S(1)}, u32[]{:S(2)}, u32[]{:S(2)}) %collective-permute-start.6) | collective-permute-done | bytes 262176 | tf_op jit(solution)/shard_map/ppermute | solution.py:324
  89.9 4.2 %collective-permute-done.7.there = bf16[128,512]{1,0:T(8,128)(2,1)S(1)} collective-permute-done((bf16[128,512]{1,0:T(8,128)(2,1)S(1)}, bf16[128,512]{1,0:T(8,128)(2,1)S(1)}, u32[]{:S(2)}, u32[]{:S(2)}) %collective-permute-start.7) | collective-permute-done | bytes 131104 | tf_op jit(solution)/shard_map/ppermute | solution.py:324
  94.1 4.2 %shard_map.96 = (bf16[128,256]{1,0:T(8,128)(2,1)S(1)}, bf16[128,256]{1,0:T(8,128)(2,1)S(1)}, bf16[128,256]{1,0:T(8,128)(2,1)S(1)}, bf16[128,256]{1,0:T(8,128)(2,1)S(1)}) custom-call(bf16[3,128,256]{2,1,0:T(8,128)(2,1)S(1)} %copy-done.7, bf16[3,128,256]{2,1,0:T(8,128)(2,1)} %collective-permute-done.22.refs_1_, bf16[3,128,256]{2,1,0:T(8,128)(2,1)S(1)} %copy-done.9, ...), custom_call_target="tpu_custom_call" | custom-call | flops 536870912 | bytes 1572864 | tf_op jit(solution)/shard_map/pallas_call | solution.py:128
  98.2 5.3 %collective-permute-start.29 = (bf16[128,256]{1,0:T(8,128)(2,1)S(1)}, bf16[128,256]{1,0:T(8,128)(2,1)S(1)}, u32[]{:S(2)}, u32[]{:S(2)}) collective-permute-start(bf16[128,256]{1,0:T(8,128)(2,1)S(1)} %get-tuple-element.38), channel_id=1, source_target_pairs={{0,4},{4,0},{8,12},{12,8},{1,5},{5,1},{9,13},{13,9},{2,6},{6,2},{1... | collective-permute-start | bytes 196616 | tf_op jit(solution)/shard_map/ppermute | solution.py:328
  103.5 5.7 %shard_map.94 = (bf16[128,384]{1,0:T(8,128)(2,1)S(1)}, bf16[128,384]{1,0:T(8,128)(2,1)S(1)}, bf16[128,384]{1,0:T(8,128)(2,1)S(1)}, bf16[128,384]{1,0:T(8,128)(2,1)S(1)}) custom-call(bf16[3,128,384]{2,1,0:T(8,128)(2,1)S(1)} %get-tuple-element.25.refs_0_, bf16[3,128,384]{2,1,0:T(8,128)(2,1)S(1)} %collective-permute-done.12.refs_1_, ...), custom_call_target="tpu_custom_call" | custom-call | flops 805306368 | bytes 2359296 | tf_op jit(solution)/shard_map/pallas_call | solution.py:128
  109.4 2.4 %collective-permute-start.31 = (bf16[128,256]{1,0:T(8,128)(2,1)S(1)}, bf16[128,256]{1,0:T(8,128)(2,1)S(1)}, u32[]{:S(2)}, u32[]{:S(2)}) collective-permute-start(bf16[128,256]{1,0:T(8,128)(2,1)S(1)} %get-tuple-element.40), channel_id=1, source_target_pairs={{0,12},{4,8},{8,4},{12,0},{1,13},{5,9},{9,5},{13,1},{2,14},{6,10},... | collective-permute-start | bytes 196616 | tf_op jit(solution)/shard_map/ppermute | solution.py:328
  113.8 2.3 %collective-permute-start.21 = (bf16[128,384]{1,0:T(8,128)(2,1)S(1)}, bf16[128,384]{1,0:T(8,128)(2,1)S(1)}, u32[]{:S(2)}, u32[]{:S(2)}) collective-permute-start(bf16[128,384]{1,0:T(8,128)(2,1)S(1)} %get-tuple-element.32), channel_id=1, source_target_pairs={{0,12},{4,8},{8,4},{12,0},{1,13},{5,9},{9,5},{13,1},{2,14},{6,10},... | collective-permute-start | bytes 294920 | tf_op jit(solution)/shard_map/ppermute | solution.py:328
  116.1 6.0 %shard_map.92.cross = f32[128,2560]{1,0:T(8,128)S(1)} custom-call(s32[1]{0:T(128)} %bitcast.1.aligned, bf16[128,512]{1,0:T(8,128)(2,1)S(1)} %add_convert_fusion.here, bf16[128,512]{1,0:T(8,128)(2,1)S(1)} %collective-permute-done.7.there, bf16[128,512]{1,0:T(8,128)(2,1)S(1)} %collective-permute-done.8.peer_here, ...), custom_call_target="tpu_custom_call" | custom-call | flops 3019898880 | bytes 11665408 | tf_op jit(solution)/shard_map/pallas_call | solution.py:128
  122.2 2.6 %collective-permute-done.20.refs_2_ = bf16[128,384]{1,0:T(8,128)(2,1)S(1)} collective-permute-done((bf16[128,384]{1,0:T(8,128)(2,1)S(1)}, bf16[128,384]{1,0:T(8,128)(2,1)S(1)}, u32[]{:S(2)}, u32[]{:S(2)}) %collective-permute-start.20) | collective-permute-done | bytes 98336 | tf_op jit(solution)/shard_map/ppermute | solution.py:328
  (78 shorter events, 17.5 us)
Async XLA Ops:
  0.0 73.1 %collective-permute-start.4 = (bf16[512,2048]{1,0:T(8,128)(2,1)}, bf16[512,2048]{1,0:T(8,128)(2,1)}, u32[]{:S(2)}, u32[]{:S(2)}) collective-permute-start(bf16[512,2048]{1,0:T(8,128)(2,1)} %refs_0_.3), channel_id=1, source_target_pairs={{0,1},{1,0},{2,3},{3,2},{4,5},{5,4},{6,7},{7,6},{8,9},{9,8},{10,11... | collective-permute-start | bytes 6291464 | tf_op jit(solution)/shard_map/ppermute | solution.py:324
  0.5 72.7 %collective-permute-start.5 = (bf16[512,2048]{1,0:T(8,128)(2,1)}, bf16[512,2048]{1,0:T(8,128)(2,1)}, u32[]{:S(2)}, u32[]{:S(2)}) collective-permute-start(bf16[512,2048]{1,0:T(8,128)(2,1)} %refs_2_.3), channel_id=1, source_target_pairs={{0,1},{1,0},{2,3},{3,2},{4,5},{5,4},{6,7},{7,6},{8,9},{9,8},{10,11... | collective-permute-start | bytes 6291464 | tf_op jit(solution)/shard_map/ppermute | solution.py:324
  6.5 106.3 %collective-permute-start.10 = (bf16[512,2560]{1,0:T(8,128)(2,1)}, bf16[512,2560]{1,0:T(8,128)(2,1)S(1)}, u32[]{:S(2)}, u32[]{:S(2)}) collective-permute-start(bf16[512,2560]{1,0:T(8,128)(2,1)} %key_near.1), channel_id=1, source_target_pairs={{0,1},{1,0},{2,3},{3,2},{4,5},{5,4},{6,7},{7,6},{8,9},{9,8},{10,11... | collective-permute-start | bytes 7864328 | tf_op jit(solution)/shard_map/ppermute | solution.py:324
  9.3 104.5 %collective-permute-start.11 = (bf16[512,2560]{1,0:T(8,128)(2,1)}, bf16[512,2560]{1,0:T(8,128)(2,1)}, u32[]{:S(2)}, u32[]{:S(2)}) collective-permute-start(bf16[512,2560]{1,0:T(8,128)(2,1)} %value_near.1), channel_id=1, source_target_pairs={{0,1},{1,0},{2,3},{3,2},{4,5},{5,4},{6,7},{7,6},{8,9},{9,8},{10,11... | collective-permute-start | bytes 7864328 | tf_op jit(solution)/shard_map/ppermute | solution.py:324
  17.2 5.8 %collective-permute-start.22 = (bf16[3,128,256]{2,1,0:T(8,128)(2,1)S(1)}, bf16[3,128,256]{2,1,0:T(8,128)(2,1)}, u32[]{:S(2)}, u32[]{:S(2)}) collective-permute-start(bf16[3,128,256]{2,1,0:T(8,128)(2,1)S(1)} %get-tuple-element.34), channel_id=1, source_target_pairs={{0,4},{4,0},{8,12},{12,8},{1,5},{5,1},{9,13},{13,9},{2,6},{6,2},{1... | collective-permute-start | bytes 589832 | tf_op jit(solution)/shard_map/ppermute | solution.py:328
  23.0 10.0 %collective-permute-start.23 = (bf16[3,128,256]{2,1,0:T(8,128)(2,1)S(1)}, bf16[3,128,256]{2,1,0:T(8,128)(2,1)S(1)}, u32[]{:S(2)}, u32[]{:S(2)}) collective-permute-start(bf16[3,128,256]{2,1,0:T(8,128)(2,1)S(1)} %get-tuple-element.35), channel_id=1, source_target_pairs={{0,8},{4,12},{8,0},{12,4},{1,9},{5,13},{9,1},{13,5},{2,10},{6,14},... | collective-permute-start | bytes 589832 | tf_op jit(solution)/shard_map/ppermute | solution.py:328
  33.0 7.5 %collective-permute-start.24 = (bf16[3,128,256]{2,1,0:T(8,128)(2,1)S(1)}, bf16[3,128,256]{2,1,0:T(8,128)(2,1)S(1)}, u32[]{:S(2)}, u32[]{:S(2)}) collective-permute-start(bf16[3,128,256]{2,1,0:T(8,128)(2,1)S(1)} %get-tuple-element.36), channel_id=1, source_target_pairs={{0,12},{4,8},{8,4},{12,0},{1,13},{5,9},{9,5},{13,1},{2,14},{6,10},... | collective-permute-start | bytes 589832 | tf_op jit(solution)/shard_map/ppermute | solution.py:328
  44.1 9.4 %collective-permute-start.12 = (bf16[3,128,384]{2,1,0:T(8,128)(2,1)S(1)}, bf16[3,128,384]{2,1,0:T(8,128)(2,1)S(1)}, u32[]{:S(2)}, u32[]{:S(2)}) collective-permute-start(bf16[3,128,384]{2,1,0:T(8,128)(2,1)S(1)} %get-tuple-element.26), channel_id=1, source_target_pairs={{0,4},{4,0},{8,12},{12,8},{1,5},{5,1},{9,13},{13,9},{2,6},{6,2},{1... | collective-permute-start | bytes 884744 | tf_op jit(solution)/shard_map/ppermute | solution.py:328
  53.5 16.1 %collective-permute-start.13 = (bf16[3,128,384]{2,1,0:T(8,128)(2,1)S(1)}, bf16[3,128,384]{2,1,0:T(8,128)(2,1)S(1)}, u32[]{:S(2)}, u32[]{:S(2)}) collective-permute-start(bf16[3,128,384]{2,1,0:T(8,128)(2,1)S(1)} %get-tuple-element.27), channel_id=1, source_target_pairs={{0,8},{4,12},{8,0},{12,4},{1,9},{5,13},{9,1},{13,5},{2,10},{6,14},... | collective-permute-start | bytes 884744 | tf_op jit(solution)/shard_map/ppermute | solution.py:328
  69.5 11.1 %collective-permute-start.14 = (bf16[3,128,384]{2,1,0:T(8,128)(2,1)}, bf16[3,128,384]{2,1,0:T(8,128)(2,1)}, u32[]{:S(2)}, u32[]{:S(2)}) collective-permute-start(bf16[3,128,384]{2,1,0:T(8,128)(2,1)} %get-tuple-element.28), channel_id=1, source_target_pairs={{0,12},{4,8},{8,4},{12,0},{1,13},{5,9},{9,5},{13,1},{2,14},{6,10},... | collective-permute-start | bytes 884744 | tf_op jit(solution)/shard_map/ppermute | solution.py:328
  73.1 9.1 %collective-permute-start.15 = (bf16[3,128,384]{2,1,0:T(8,128)(2,1)S(1)}, bf16[3,128,384]{2,1,0:T(8,128)(2,1)}, u32[]{:S(2)}, u32[]{:S(2)}) collective-permute-start(bf16[3,128,384]{2,1,0:T(8,128)(2,1)S(1)} %get-tuple-element.25.refs_0_), channel_id=1, source_target_pairs={{0,1},{1,0},{2,3},{3,2},{4,5},{5,4},{6,7},{7,6},{8,9},{9,8},{10,11... | collective-permute-start | bytes 884744 | tf_op jit(solution)/shard_map/ppermute | solution.py:324
  73.2 9.0 %collective-permute-start.26 = (bf16[3,128,256]{2,1,0:T(8,128)(2,1)}, bf16[3,128,256]{2,1,0:T(8,128)(2,1)}, u32[]{:S(2)}, u32[]{:S(2)}) collective-permute-start(bf16[3,128,256]{2,1,0:T(8,128)(2,1)} %collective-permute-done.22.refs_1_), channel_id=1, source_target_pairs={{0,1},{1,0},{2,3},{3,2},{4,5},{5,4},{6,7},{7,6},{8,9},{9,8},{10,11... | collective-permute-start | bytes 589832 | tf_op jit(solution)/shard_map/ppermute | solution.py:324
  80.7 7.3 %collective-permute-start.6 = (f32[128,512]{1,0:T(8,128)S(1)}, f32[128,512]{1,0:T(8,128)S(1)}, u32[]{:S(2)}, u32[]{:S(2)}) collective-permute-start(f32[128,512]{1,0:T(8,128)S(1)} %get-tuple-element.24), channel_id=1, source_target_pairs={{0,2},{2,0},{1,3},{3,1},{4,6},{6,4},{5,7},{7,5},{8,10},{10,8},{9,1... | collective-permute-start | bytes 786440 | tf_op jit(solution)/shard_map/ppermute | solution.py:324
  83.9 5.7 %collective-permute-start.17 = (bf16[3,128,384]{2,1,0:T(8,128)(2,1)S(1)}, bf16[3,128,384]{2,1,0:T(8,128)(2,1)S(1)}, u32[]{:S(2)}, u32[]{:S(2)}) collective-permute-start(bf16[3,128,384]{2,1,0:T(8,128)(2,1)S(1)} %copy-done.5), channel_id=1, source_target_pairs={{0,1},{1,0},{2,3},{3,2},{4,5},{5,4},{6,7},{7,6},{8,9},{9,8},{10,11... | collective-permute-start | bytes 884744 | tf_op jit(solution)/shard_map/ppermute | solution.py:324
  88.0 10.2 %collective-permute-start.18 = (bf16[3,128,384]{2,1,0:T(8,128)(2,1)}, bf16[3,128,384]{2,1,0:T(8,128)(2,1)S(1)}, u32[]{:S(2)}, u32[]{:S(2)}) collective-permute-start(bf16[3,128,384]{2,1,0:T(8,128)(2,1)} %collective-permute-done.14.refs_3_), channel_id=1, source_target_pairs={{0,1},{1,0},{2,3},{3,2},{4,5},{5,4},{6,7},{7,6},{8,9},{9,8},{10,11... | collective-permute-start | bytes 884744 | tf_op jit(solution)/shard_map/ppermute | solution.py:324
  88.1 6.0 %collective-permute-start.7 = (bf16[128,512]{1,0:T(8,128)(2,1)S(1)}, bf16[128,512]{1,0:T(8,128)(2,1)S(1)}, u32[]{:S(2)}, u32[]{:S(2)}) collective-permute-start(bf16[128,512]{1,0:T(8,128)(2,1)S(1)} %add_convert_fusion.here), channel_id=1, source_target_pairs={{0,2},{2,0},{1,3},{3,1},{4,6},{6,4},{5,7},{7,5},{8,10},{10,8},{9,1... | collective-permute-start | bytes 393224 | tf_op jit(solution)/shard_map/ppermute | solution.py:324
  89.6 19.7 %collective-permute-start.8 = (bf16[128,512]{1,0:T(8,128)(2,1)S(1)}, bf16[128,512]{1,0:T(8,128)(2,1)S(1)}, u32[]{:S(2)}, u32[]{:S(2)}) collective-permute-start(bf16[128,512]{1,0:T(8,128)(2,1)S(1)} %add_convert_fusion.here), channel_id=1, source_target_pairs={{0,1},{1,0},{2,3},{3,2},{4,5},{5,4},{6,7},{7,6},{8,9},{9,8},{10,11... | collective-permute-start | bytes 393224 | tf_op jit(solution)/shard_map/ppermute | solution.py:324
  94.1 17.7 %collective-permute-start.9 = (bf16[128,512]{1,0:T(8,128)(2,1)S(1)}, bf16[128,512]{1,0:T(8,128)(2,1)S(1)}, u32[]{:S(2)}, u32[]{:S(2)}) collective-permute-start(bf16[128,512]{1,0:T(8,128)(2,1)S(1)} %collective-permute-done.7.there), channel_id=1, source_target_pairs={{0,1},{1,0},{2,3},{3,2},{4,5},{5,4},{6,7},{7,6},{8,9},{9,8},{10,11... | collective-permute-start | bytes 393224 | tf_op jit(solution)/shard_map/ppermute | solution.py:324
  98.2 11.0 %collective-permute-start.29 = (bf16[128,256]{1,0:T(8,128)(2,1)S(1)}, bf16[128,256]{1,0:T(8,128)(2,1)S(1)}, u32[]{:S(2)}, u32[]{:S(2)}) collective-permute-start(bf16[128,256]{1,0:T(8,128)(2,1)S(1)} %get-tuple-element.38), channel_id=1, source_target_pairs={{0,4},{4,0},{8,12},{12,8},{1,5},{5,1},{9,13},{13,9},{2,6},{6,2},{1... | collective-permute-start | bytes 196616 | tf_op jit(solution)/shard_map/ppermute | solution.py:328
  109.3 12.9 %collective-permute-start.30 = (bf16[128,256]{1,0:T(8,128)(2,1)S(1)}, bf16[128,256]{1,0:T(8,128)(2,1)S(1)}, u32[]{:S(2)}, u32[]{:S(2)}) collective-permute-start(bf16[128,256]{1,0:T(8,128)(2,1)S(1)} %get-tuple-element.39), channel_id=1, source_target_pairs={{0,8},{4,12},{8,0},{12,4},{1,9},{5,13},{9,1},{13,5},{2,10},{6,14},... | collective-permute-start | bytes 196616 | tf_op jit(solution)/shard_map/ppermute | solution.py:328
  109.4 12.8 %collective-permute-start.31 = (bf16[128,256]{1,0:T(8,128)(2,1)S(1)}, bf16[128,256]{1,0:T(8,128)(2,1)S(1)}, u32[]{:S(2)}, u32[]{:S(2)}) collective-permute-start(bf16[128,256]{1,0:T(8,128)(2,1)S(1)} %get-tuple-element.40), channel_id=1, source_target_pairs={{0,12},{4,8},{8,4},{12,0},{1,13},{5,9},{9,5},{13,1},{2,14},{6,10},... | collective-permute-start | bytes 196616 | tf_op jit(solution)/shard_map/ppermute | solution.py:328
  111.7 10.5 %collective-permute-start.19 = (bf16[128,384]{1,0:T(8,128)(2,1)S(1)}, bf16[128,384]{1,0:T(8,128)(2,1)S(1)}, u32[]{:S(2)}, u32[]{:S(2)}) collective-permute-start(bf16[128,384]{1,0:T(8,128)(2,1)S(1)} %get-tuple-element.30), channel_id=1, source_target_pairs={{0,4},{4,0},{8,12},{12,8},{1,5},{5,1},{9,13},{13,9},{2,6},{6,2},{1... | collective-permute-start | bytes 294920 | tf_op jit(solution)/shard_map/ppermute | solution.py:328
  112.8 12.0 %collective-permute-start.20 = (bf16[128,384]{1,0:T(8,128)(2,1)S(1)}, bf16[128,384]{1,0:T(8,128)(2,1)S(1)}, u32[]{:S(2)}, u32[]{:S(2)}) collective-permute-start(bf16[128,384]{1,0:T(8,128)(2,1)S(1)} %get-tuple-element.31), channel_id=1, source_target_pairs={{0,8},{4,12},{8,0},{12,4},{1,9},{5,13},{9,1},{13,5},{2,10},{6,14},... | collective-permute-start | bytes 294920 | tf_op jit(solution)/shard_map/ppermute | solution.py:328
  113.8 11.0 %collective-permute-start.21 = (bf16[128,384]{1,0:T(8,128)(2,1)S(1)}, bf16[128,384]{1,0:T(8,128)(2,1)S(1)}, u32[]{:S(2)}, u32[]{:S(2)}) collective-permute-start(bf16[128,384]{1,0:T(8,128)(2,1)S(1)} %get-tuple-element.32), channel_id=1, source_target_pairs={{0,12},{4,8},{8,4},{12,0},{1,13},{5,9},{9,5},{13,1},{2,14},{6,10},... | collective-permute-start | bytes 294920 | tf_op jit(solution)/shard_map/ppermute | solution.py:328
  (22 other events, 269.5 us)

commit v2 on v1

--- a/solution.py
+++ b/solution.py
@@ -150,13 +150,14 @@
     return pl.ds(pl.multiple_of(head * HEAD_DIM, HEAD_DIM), HEAD_DIM)
 
 
-def pack_kernel(views, offset, view, *refs):
-    sources, results, arrived = refs[:3], refs[3:-1], refs[-1]
+def pack_kernel(views, offset, view, side, *refs):
+    count = (len(refs) - 1 - views + 3) // 2
+    sources, results, arrived = refs[:count], refs[count:-1], refs[-1]
     span = sources[0].shape[1] // views
     copies = []
-    for step, result in enumerate(results):
+    for step, result in enumerate(results[:views]):
         start = pl.multiple_of((view[0] ^ step) * span + offset, HEAD_DIM)
-        for slot, source in enumerate(sources):
+        for slot, source in enumerate(sources[:3]):
             copies.append(
                 pltpu.make_async_copy(
                     source.at[:, pl.ds(start, result.shape[2])],
@@ -164,23 +165,31 @@
                     arrived.at[step, slot],
                 )
             )
+    for source, result in zip(sources[3:], results[views:]):
+        half = result.shape[1]
+        start = pl.multiple_of(side[0] * half, HEAD_DIM)
+        copies.append(
+            pltpu.make_async_copy(source.at[:, pl.ds(start, half)], result, arrived.at[views, 0])
+        )
     for copy in copies:
         copy.start()
     for copy in copies:
         copy.wait()
 
 
-def pack(view, views, offset, width, keys, values, queries):
+def pack(view, side, views, offset, width, keys, values, queries, *rays):
     rows = keys.shape[0]
+    out_shape = [jax.ShapeDtypeStruct((3, rows, width), jnp.bfloat16)] * views
+    out_shape += [jax.ShapeDtypeStruct((r.shape[0], r.shape[1] // 2), r.dtype) for r in rays]
     return local_call(
         functools.partial(pack_kernel, views, offset),
         8,
         keys.size,
         0,
-        [jax.ShapeDtypeStruct((3, rows, width), jnp.bfloat16)] * views,
-        (view,),
-        streamed=(keys, values, queries),
-        scratch=(pltpu.SemaphoreType.DMA((views, 3)),),
+        out_shape,
+        (view, side),
+        streamed=(keys, values, queries, *rays),
+        scratch=(pltpu.SemaphoreType.DMA((views + 1, 3)),),
     )
 
 
@@ -349,8 +358,13 @@
     widths, offsets = chunk_columns(span)
     aligned = side == core
 
-    half = ray_tokens.shape[1] // 2
-    ray_half = lax.dynamic_slice(ray_tokens, (0, side * half), (ray_tokens.shape[0], half))
+    packed = []
+    for index, columns in enumerate(zip(offsets, widths)):
+        extra = () if index else (ray_tokens,)
+        packed.append(
+            pack(view, side, views, *columns, video_keys, video_values, video_queries, *extra)
+        )
+    ray_half = packed[0][views]
     ray_rows = jnp.concatenate(
         [ray_half]
         + [exchanged(ray_half, views, step) for step in range(1, views)],
@@ -361,12 +375,11 @@
     key_peer = swapped(key_weight, "dp")
     value_peer = swapped(value_weight, "dp")
 
-    packed = [
-        pack(view, views, *columns, video_keys, video_values, video_queries)
-        for columns in zip(offsets, widths)
-    ]
     chunks = [
-        [exchanged(piece, views, step) if step else piece for step, piece in enumerate(pieces)]
+        [
+            exchanged(piece, views, step) if step else piece
+            for step, piece in enumerate(pieces[:views])
+        ]
         for pieces in packed
     ]
 

time: 126 us -> 124 us (0.984)
  starting transfers between devices: 36 us -> 30.2 us
  waiting for transfers between devices: 62.5 us -> 65.2 us
    ppermute x15, starting transfers between devices: 29.2 us -> 23.6 us  [exchanged(): return lax.ppermute(values, 'view', [(i, i ^ step) for i in range(views)])]
    ppermute x17, waiting for transfers between devices: 11.3 us -> 13 us  [swapped(): return lax.ppermute(values, axis, [(0, 1), (1, 0)])]
    unnamed x28 -> x31, local copies, waits for them, and re-layouts: 1.69 us -> 2.82 us
  transfers between devices with their start and end apart: 32 -> 32, of which waited for: 14 -> 15; matrix products, arithmetic and copies ran while one was open for 0% -> 0% of each run, Pallas kernels for 19% -> 20%
where the time goes in v2:
time: 124 us
  waiting for transfers between devices  65.2 us (53%)
  starting transfers between devices  30.2 us (24%)
  Pallas kernels  25.3 us (20%)
  local copies, waits for them, and re-layouts  2.83 us (2%)
    ppermute x15, waiting for transfers between devices, exchanged(): return lax.ppermute(values, 'view', [(i, i ^ step) for i in range(views)])  52.3 us
    pallas_call x7, Pallas kernels, local_call(): return call(*scalars, *arrays, *streamed)  25.3 us
    ppermute x15, starting transfers between devices, exchanged(): return lax.ppermute(values, 'view', [(i, i ^ step) for i in range(views)])  23.6 us
    ppermute x17, waiting for transfers between devices, swapped(): return lax.ppermute(values, axis, [(0, 1), (1, 0)])  13 us
    ppermute x17, starting transfers between devices, swapped(): return lax.ppermute(values, axis, [(0, 1), (1, 0)])  6.68 us
    unnamed x31, local copies, waits for them, and re-layouts  2.82 us
  transfers between devices with their start and end apart: 32, of which 15 were waited for; matrix products, arithmetic and copies ran while one was open for 0% of the time, Pallas kernels for 20%

profile of v2, /device:TPU:0, one launch (start us, length us, event | category | flops | bytes accessed | tf_op | source)
XLA Modules:
  0.0 123.9 jit_solution(3046094467482599173)
XLA Ops:
  0.5 2.2 %shard_map.91 = (bf16[3,128,384]{2,1,0:T(8,128)(2,1)S(1)}, bf16[3,128,384]{2,1,0:T(8,128)(2,1)S(1)}, bf16[3,128,384]{2,1,0:T(8,128)(2,1)S(1)}, bf16[3,128,384]{2,1,0:T(8,128)(2,1)}, bf16[32,512]{1,0:T(8,128)(2,1)S(1)}) custom-call(s32[1]{0:T(128)} %bitcast.view, s32[1]{0:T(128)} %bitcast.2.side, bf16[128,2560]{1,0:T(8,128)(2,1)} %refs_0_.5, ...), custom_call_target="tpu_custom_call" | custom-call | flops 327680 | bytes 2031616 | tf_op jit(solution)/shard_map/pallas_call | solution.py:128
  2.7 4.7 %collective-permute-start.2 = (bf16[32,512]{1,0:T(8,128)(2,1)S(1)}, bf16[32,512]{1,0:T(8,128)(2,1)S(1)}, u32[]{:S(2)}, u32[]{:S(2)}) collective-permute-start(bf16[32,512]{1,0:T(8,128)(2,1)S(1)} %get-tuple-element.24), channel_id=1, source_target_pairs={{0,12},{4,8},{8,4},{12,0},{1,13},{5,9},{9,5},{13,1},{2,14},{6,10},... | collective-permute-start | bytes 98312 | tf_op jit(solution)/shard_map/ppermute | solution.py:337
  8.0 3.6 %collective-permute-done = bf16[32,512]{1,0:T(8,128)(2,1)S(1)} collective-permute-done((bf16[32,512]{1,0:T(8,128)(2,1)S(1)}, bf16[32,512]{1,0:T(8,128)(2,1)S(1)}, u32[]{:S(2)}, u32[]{:S(2)}) %collective-permute-start) | collective-permute-done | bytes 32800 | tf_op jit(solution)/shard_map/ppermute | solution.py:337
  15.0 3.1 %collective-permute-done.3.there_ref = bf16[128,512]{1,0:T(8,128)(2,1)S(1)} collective-permute-done((bf16[128,512]{1,0:T(8,128)(2,1)S(1)}, bf16[128,512]{1,0:T(8,128)(2,1)S(1)}, u32[]{:S(2)}, u32[]{:S(2)}) %collective-permute-start.3) | collective-permute-done | bytes 131104 | tf_op jit(solution)/shard_map/ppermute | solution.py:333
  18.6 6.1 %collective-permute-done.22.refs_1_ = bf16[3,128,256]{2,1,0:T(8,128)(2,1)} collective-permute-done((bf16[3,128,256]{2,1,0:T(8,128)(2,1)S(1)}, bf16[3,128,256]{2,1,0:T(8,128)(2,1)}, u32[]{:S(2)}, u32[]{:S(2)}) %collective-permute-start.22) | collective-permute-done | bytes 196640 | tf_op jit(solution)/shard_map/ppermute | solution.py:337
  24.7 1.7 %collective-permute-start.23 = (bf16[3,128,256]{2,1,0:T(8,128)(2,1)S(1)}, bf16[3,128,256]{2,1,0:T(8,128)(2,1)S(1)}, u32[]{:S(2)}, u32[]{:S(2)}) collective-permute-start(bf16[3,128,256]{2,1,0:T(8,128)(2,1)S(1)} %get-tuple-element.37), channel_id=1, source_target_pairs={{0,8},{4,12},{8,0},{12,4},{1,9},{5,13},{9,1},{13,5},{2,10},{6,14},... | collective-permute-start | bytes 589832 | tf_op jit(solution)/shard_map/ppermute | solution.py:337
  26.4 8.6 %collective-permute-done.23.refs_2_ = bf16[3,128,256]{2,1,0:T(8,128)(2,1)S(1)} collective-permute-done((bf16[3,128,256]{2,1,0:T(8,128)(2,1)S(1)}, bf16[3,128,256]{2,1,0:T(8,128)(2,1)S(1)}, u32[]{:S(2)}, u32[]{:S(2)}) %collective-permute-start.23) | collective-permute-done | bytes 196640 | tf_op jit(solution)/shard_map/ppermute | solution.py:337
  34.9 1.7 %collective-permute-start.24 = (bf16[3,128,256]{2,1,0:T(8,128)(2,1)S(1)}, bf16[3,128,256]{2,1,0:T(8,128)(2,1)S(1)}, u32[]{:S(2)}, u32[]{:S(2)}) collective-permute-start(bf16[3,128,256]{2,1,0:T(8,128)(2,1)S(1)} %get-tuple-element.38), channel_id=1, source_target_pairs={{0,12},{4,8},{8,4},{12,0},{1,13},{5,9},{9,5},{13,1},{2,14},{6,10},... | collective-permute-start | bytes 589832 | tf_op jit(solution)/shard_map/ppermute | solution.py:337
  36.6 6.9 %collective-permute-done.24.refs_3_ = bf16[3,128,256]{2,1,0:T(8,128)(2,1)S(1)} collective-permute-done((bf16[3,128,256]{2,1,0:T(8,128)(2,1)S(1)}, bf16[3,128,256]{2,1,0:T(8,128)(2,1)S(1)}, u32[]{:S(2)}, u32[]{:S(2)}) %collective-permute-start.24) | collective-permute-done | bytes 196640 | tf_op jit(solution)/shard_map/ppermute | solution.py:337
  46.3 8.4 %collective-permute-done.12.refs_1_ = bf16[3,128,384]{2,1,0:T(8,128)(2,1)S(1)} collective-permute-done((bf16[3,128,384]{2,1,0:T(8,128)(2,1)S(1)}, bf16[3,128,384]{2,1,0:T(8,128)(2,1)S(1)}, u32[]{:S(2)}, u32[]{:S(2)}) %collective-permute-start.12) | collective-permute-done | bytes 294944 | tf_op jit(solution)/shard_map/ppermute | solution.py:337
  54.7 1.9 %collective-permute-start.13 = (bf16[3,128,384]{2,1,0:T(8,128)(2,1)S(1)}, bf16[3,128,384]{2,1,0:T(8,128)(2,1)S(1)}, u32[]{:S(2)}, u32[]{:S(2)}) collective-permute-start(bf16[3,128,384]{2,1,0:T(8,128)(2,1)S(1)} %get-tuple-element.29), channel_id=1, source_target_pairs={{0,8},{4,12},{8,0},{12,4},{1,9},{5,13},{9,1},{13,5},{2,10},{6,14},... | collective-permute-start | bytes 884744 | tf_op jit(solution)/shard_map/ppermute | solution.py:337
  56.5 13.6 %collective-permute-done.13.refs_2_ = bf16[3,128,384]{2,1,0:T(8,128)(2,1)S(1)} collective-permute-done((bf16[3,128,384]{2,1,0:T(8,128)(2,1)S(1)}, bf16[3,128,384]{2,1,0:T(8,128)(2,1)S(1)}, u32[]{:S(2)}, u32[]{:S(2)}) %collective-permute-start.13) | collective-permute-done | bytes 294944 | tf_op jit(solution)/shard_map/ppermute | solution.py:337
  70.1 1.9 %collective-permute-start.14 = (bf16[3,128,384]{2,1,0:T(8,128)(2,1)}, bf16[3,128,384]{2,1,0:T(8,128)(2,1)}, u32[]{:S(2)}, u32[]{:S(2)}) collective-permute-start(bf16[3,128,384]{2,1,0:T(8,128)(2,1)} %get-tuple-element.30), channel_id=1, source_target_pairs={{0,12},{4,8},{8,4},{12,0},{1,13},{5,9},{9,5},{13,1},{2,14},{6,10},... | collective-permute-start | bytes 884744 | tf_op jit(solution)/shard_map/ppermute | solution.py:337
  73.9 4.9 %shard_map.92 = (f32[128,512]{1,0:T(8,128)S(1)}, f32[128,512]{1,0:T(8,128)S(1)}) custom-call(s32[1]{0:T(128)} %bitcast.1.aligned, bf16[128,512]{1,0:T(8,128)(2,1)S(1)} %constant_dynamic-update-slice_fusion.here_ref, bf16[128,512]{1,0:T(8,128)(2,1)S(1)} %collective-permute-done.3.there_ref, bf16[512,2048]{1,0:T(8,128)(2,1)} %refs_0_.4, ...), custom_call_target="tpu_custom_call" | custom-call | flops 1073741824 | bytes 8650752 | tf_op jit(solution)/shard_map/pallas_call | solution.py:128
  78.9 2.2 %collective-permute-done.14.refs_3_ = bf16[3,128,384]{2,1,0:T(8,128)(2,1)} collective-permute-done((bf16[3,128,384]{2,1,0:T(8,128)(2,1)}, bf16[3,128,384]{2,1,0:T(8,128)(2,1)}, u32[]{:S(2)}, u32[]{:S(2)}) %collective-permute-start.14) | collective-permute-done | bytes 294944 | tf_op jit(solution)/shard_map/ppermute | solution.py:337
  84.5 3.8 %collective-permute-done.6 = f32[128,512]{1,0:T(8,128)S(1)} collective-permute-done((f32[128,512]{1,0:T(8,128)S(1)}, f32[128,512]{1,0:T(8,128)S(1)}, u32[]{:S(2)}, u32[]{:S(2)}) %collective-permute-start.6) | collective-permute-done | bytes 262176 | tf_op jit(solution)/shard_map/ppermute | solution.py:333
  90.2 4.2 %collective-permute-done.7.there = bf16[128,512]{1,0:T(8,128)(2,1)S(1)} collective-permute-done((bf16[128,512]{1,0:T(8,128)(2,1)S(1)}, bf16[128,512]{1,0:T(8,128)(2,1)S(1)}, u32[]{:S(2)}, u32[]{:S(2)}) %collective-permute-start.7) | collective-permute-done | bytes 131104 | tf_op jit(solution)/shard_map/ppermute | solution.py:333
  94.4 4.2 %shard_map.96 = (bf16[128,256]{1,0:T(8,128)(2,1)S(1)}, bf16[128,256]{1,0:T(8,128)(2,1)S(1)}, bf16[128,256]{1,0:T(8,128)(2,1)S(1)}, bf16[128,256]{1,0:T(8,128)(2,1)S(1)}) custom-call(bf16[3,128,256]{2,1,0:T(8,128)(2,1)S(1)} %copy-done.6, bf16[3,128,256]{2,1,0:T(8,128)(2,1)} %collective-permute-done.22.refs_1_, bf16[3,128,256]{2,1,0:T(8,128)(2,1)S(1)} %copy-done.8, ...), custom_call_target="tpu_custom_call" | custom-call | flops 536870912 | bytes 1572864 | tf_op jit(solution)/shard_map/pallas_call | solution.py:128
  98.6 2.2 %collective-permute-start.29 = (bf16[128,256]{1,0:T(8,128)(2,1)S(1)}, bf16[128,256]{1,0:T(8,128)(2,1)S(1)}, u32[]{:S(2)}, u32[]{:S(2)}) collective-permute-start(bf16[128,256]{1,0:T(8,128)(2,1)S(1)} %get-tuple-element.40), channel_id=1, source_target_pairs={{0,4},{4,0},{8,12},{12,8},{1,5},{5,1},{9,13},{13,9},{2,6},{6,2},{1... | collective-permute-start | bytes 196616 | tf_op jit(solution)/shard_map/ppermute | solution.py:337
  100.8 5.7 %shard_map.94 = (bf16[128,384]{1,0:T(8,128)(2,1)S(1)}, bf16[128,384]{1,0:T(8,128)(2,1)S(1)}, bf16[128,384]{1,0:T(8,128)(2,1)S(1)}, bf16[128,384]{1,0:T(8,128)(2,1)S(1)}) custom-call(bf16[3,128,384]{2,1,0:T(8,128)(2,1)S(1)} %get-tuple-element.27.refs_0_, bf16[3,128,384]{2,1,0:T(8,128)(2,1)S(1)} %collective-permute-done.12.refs_1_, ...), custom_call_target="tpu_custom_call" | custom-call | flops 805306368 | bytes 2359296 | tf_op jit(solution)/shard_map/pallas_call | solution.py:128
  106.5 1.9 %collective-permute-start.30 = (bf16[128,256]{1,0:T(8,128)(2,1)S(1)}, bf16[128,256]{1,0:T(8,128)(2,1)S(1)}, u32[]{:S(2)}, u32[]{:S(2)}) collective-permute-start(bf16[128,256]{1,0:T(8,128)(2,1)S(1)} %get-tuple-element.41), channel_id=1, source_target_pairs={{0,8},{4,12},{8,0},{12,4},{1,9},{5,13},{9,1},{13,5},{2,10},{6,14},... | collective-permute-start | bytes 196616 | tf_op jit(solution)/shard_map/ppermute | solution.py:337
  110.6 2.3 %collective-permute-start.20 = (bf16[128,384]{1,0:T(8,128)(2,1)S(1)}, bf16[128,384]{1,0:T(8,128)(2,1)S(1)}, u32[]{:S(2)}, u32[]{:S(2)}) collective-permute-start(bf16[128,384]{1,0:T(8,128)(2,1)S(1)} %get-tuple-element.33), channel_id=1, source_target_pairs={{0,8},{4,12},{8,0},{12,4},{1,9},{5,13},{9,1},{13,5},{2,10},{6,14},... | collective-permute-start | bytes 294920 | tf_op jit(solution)/shard_map/ppermute | solution.py:337
  114.4 6.0 %shard_map.93.cross = f32[128,2560]{1,0:T(8,128)S(1)} custom-call(s32[1]{0:T(128)} %bitcast.1.aligned, bf16[128,512]{1,0:T(8,128)(2,1)S(1)} %add_convert_fusion.here, bf16[128,512]{1,0:T(8,128)(2,1)S(1)} %collective-permute-done.7.there, bf16[128,512]{1,0:T(8,128)(2,1)S(1)} %collective-permute-done.8.peer_here, ...), custom_call_target="tpu_custom_call" | custom-call | flops 3019898880 | bytes 11665408 | tf_op jit(solution)/shard_map/pallas_call | solution.py:128
  120.5 2.4 %collective-permute-done.20.refs_2_ = bf16[128,384]{1,0:T(8,128)(2,1)S(1)} collective-permute-done((bf16[128,384]{1,0:T(8,128)(2,1)S(1)}, bf16[128,384]{1,0:T(8,128)(2,1)S(1)}, u32[]{:S(2)}, u32[]{:S(2)}) %collective-permute-start.20) | collective-permute-done | bytes 98336 | tf_op jit(solution)/shard_map/ppermute | solution.py:337
  (80 shorter events, 19.6 us)
Async XLA Ops:
  0.0 72.0 %collective-permute-start.4 = (bf16[512,2048]{1,0:T(8,128)(2,1)}, bf16[512,2048]{1,0:T(8,128)(2,1)}, u32[]{:S(2)}, u32[]{:S(2)}) collective-permute-start(bf16[512,2048]{1,0:T(8,128)(2,1)} %refs_0_.4), channel_id=1, source_target_pairs={{0,1},{1,0},{2,3},{3,2},{4,5},{5,4},{6,7},{7,6},{8,9},{9,8},{10,11... | collective-permute-start | bytes 6291464 | tf_op jit(solution)/shard_map/ppermute | solution.py:333
  2.7 9.5 %collective-permute-start.2 = (bf16[32,512]{1,0:T(8,128)(2,1)S(1)}, bf16[32,512]{1,0:T(8,128)(2,1)S(1)}, u32[]{:S(2)}, u32[]{:S(2)}) collective-permute-start(bf16[32,512]{1,0:T(8,128)(2,1)S(1)} %get-tuple-element.24), channel_id=1, source_target_pairs={{0,12},{4,8},{8,4},{12,0},{1,13},{5,9},{9,5},{13,1},{2,14},{6,10},... | collective-permute-start | bytes 98312 | tf_op jit(solution)/shard_map/ppermute | solution.py:337
  8.0 64.1 %collective-permute-start.5 = (bf16[512,2048]{1,0:T(8,128)(2,1)}, bf16[512,2048]{1,0:T(8,128)(2,1)S(1)}, u32[]{:S(2)}, u32[]{:S(2)}) collective-permute-start(bf16[512,2048]{1,0:T(8,128)(2,1)} %refs_2_.4), channel_id=1, source_target_pairs={{0,1},{1,0},{2,3},{3,2},{4,5},{5,4},{6,7},{7,6},{8,9},{9,8},{10,11... | collective-permute-start | bytes 6291464 | tf_op jit(solution)/shard_map/ppermute | solution.py:333
  11.6 99.0 %collective-permute-start.10 = (bf16[512,2560]{1,0:T(8,128)(2,1)}, bf16[512,2560]{1,0:T(8,128)(2,1)S(1)}, u32[]{:S(2)}, u32[]{:S(2)}) collective-permute-start(bf16[512,2560]{1,0:T(8,128)(2,1)} %key_near.1), channel_id=1, source_target_pairs={{0,1},{1,0},{2,3},{3,2},{4,5},{5,4},{6,7},{7,6},{8,9},{9,8},{10,11... | collective-permute-start | bytes 7864328 | tf_op jit(solution)/shard_map/ppermute | solution.py:333
  12.2 100.7 %collective-permute-start.11 = (bf16[512,2560]{1,0:T(8,128)(2,1)}, bf16[512,2560]{1,0:T(8,128)(2,1)}, u32[]{:S(2)}, u32[]{:S(2)}) collective-permute-start(bf16[512,2560]{1,0:T(8,128)(2,1)} %value_near.1), channel_id=1, source_target_pairs={{0,1},{1,0},{2,3},{3,2},{4,5},{5,4},{6,7},{7,6},{8,9},{9,8},{10,11... | collective-permute-start | bytes 7864328 | tf_op jit(solution)/shard_map/ppermute | solution.py:333
  18.1 6.5 %collective-permute-start.22 = (bf16[3,128,256]{2,1,0:T(8,128)(2,1)S(1)}, bf16[3,128,256]{2,1,0:T(8,128)(2,1)}, u32[]{:S(2)}, u32[]{:S(2)}) collective-permute-start(bf16[3,128,256]{2,1,0:T(8,128)(2,1)S(1)} %get-tuple-element.36), channel_id=1, source_target_pairs={{0,4},{4,0},{8,12},{12,8},{1,5},{5,1},{9,13},{13,9},{2,6},{6,2},{1... | collective-permute-start | bytes 589832 | tf_op jit(solution)/shard_map/ppermute | solution.py:337
  24.7 10.2 %collective-permute-start.23 = (bf16[3,128,256]{2,1,0:T(8,128)(2,1)S(1)}, bf16[3,128,256]{2,1,0:T(8,128)(2,1)S(1)}, u32[]{:S(2)}, u32[]{:S(2)}) collective-permute-start(bf16[3,128,256]{2,1,0:T(8,128)(2,1)S(1)} %get-tuple-element.37), channel_id=1, source_target_pairs={{0,8},{4,12},{8,0},{12,4},{1,9},{5,13},{9,1},{13,5},{2,10},{6,14},... | collective-permute-start | bytes 589832 | tf_op jit(solution)/shard_map/ppermute | solution.py:337
  34.9 8.6 %collective-permute-start.24 = (bf16[3,128,256]{2,1,0:T(8,128)(2,1)S(1)}, bf16[3,128,256]{2,1,0:T(8,128)(2,1)S(1)}, u32[]{:S(2)}, u32[]{:S(2)}) collective-permute-start(bf16[3,128,256]{2,1,0:T(8,128)(2,1)S(1)} %get-tuple-element.38), channel_id=1, source_target_pairs={{0,12},{4,8},{8,4},{12,0},{1,13},{5,9},{9,5},{13,1},{2,14},{6,10},... | collective-permute-start | bytes 589832 | tf_op jit(solution)/shard_map/ppermute | solution.py:337
  45.6 9.1 %collective-permute-start.12 = (bf16[3,128,384]{2,1,0:T(8,128)(2,1)S(1)}, bf16[3,128,384]{2,1,0:T(8,128)(2,1)S(1)}, u32[]{:S(2)}, u32[]{:S(2)}) collective-permute-start(bf16[3,128,384]{2,1,0:T(8,128)(2,1)S(1)} %get-tuple-element.28), channel_id=1, source_target_pairs={{0,4},{4,0},{8,12},{12,8},{1,5},{5,1},{9,13},{13,9},{2,6},{6,2},{1... | collective-permute-start | bytes 884744 | tf_op jit(solution)/shard_map/ppermute | solution.py:337
  54.7 15.4 %collective-permute-start.13 = (bf16[3,128,384]{2,1,0:T(8,128)(2,1)S(1)}, bf16[3,128,384]{2,1,0:T(8,128)(2,1)S(1)}, u32[]{:S(2)}, u32[]{:S(2)}) collective-permute-start(bf16[3,128,384]{2,1,0:T(8,128)(2,1)S(1)} %get-tuple-element.29), channel_id=1, source_target_pairs={{0,8},{4,12},{8,0},{12,4},{1,9},{5,13},{9,1},{13,5},{2,10},{6,14},... | collective-permute-start | bytes 884744 | tf_op jit(solution)/shard_map/ppermute | solution.py:337
  70.1 11.0 %collective-permute-start.14 = (bf16[3,128,384]{2,1,0:T(8,128)(2,1)}, bf16[3,128,384]{2,1,0:T(8,128)(2,1)}, u32[]{:S(2)}, u32[]{:S(2)}) collective-permute-start(bf16[3,128,384]{2,1,0:T(8,128)(2,1)} %get-tuple-element.30), channel_id=1, source_target_pairs={{0,12},{4,8},{8,4},{12,0},{1,13},{5,9},{9,5},{13,1},{2,14},{6,10},... | collective-permute-start | bytes 884744 | tf_op jit(solution)/shard_map/ppermute | solution.py:337
  72.0 10.6 %collective-permute-start.15 = (bf16[3,128,384]{2,1,0:T(8,128)(2,1)S(1)}, bf16[3,128,384]{2,1,0:T(8,128)(2,1)}, u32[]{:S(2)}, u32[]{:S(2)}) collective-permute-start(bf16[3,128,384]{2,1,0:T(8,128)(2,1)S(1)} %get-tuple-element.27.refs_0_), channel_id=1, source_target_pairs={{0,1},{1,0},{2,3},{3,2},{4,5},{5,4},{6,7},{7,6},{8,9},{9,8},{10,11... | collective-permute-start | bytes 884744 | tf_op jit(solution)/shard_map/ppermute | solution.py:333
  73.4 9.2 %collective-permute-start.26 = (bf16[3,128,256]{2,1,0:T(8,128)(2,1)}, bf16[3,128,256]{2,1,0:T(8,128)(2,1)}, u32[]{:S(2)}, u32[]{:S(2)}) collective-permute-start(bf16[3,128,256]{2,1,0:T(8,128)(2,1)} %collective-permute-done.22.refs_1_), channel_id=1, source_target_pairs={{0,1},{1,0},{2,3},{3,2},{4,5},{5,4},{6,7},{7,6},{8,9},{9,8},{10,11... | collective-permute-start | bytes 589832 | tf_op jit(solution)/shard_map/ppermute | solution.py:333
  81.1 7.2 %collective-permute-start.6 = (f32[128,512]{1,0:T(8,128)S(1)}, f32[128,512]{1,0:T(8,128)S(1)}, u32[]{:S(2)}, u32[]{:S(2)}) collective-permute-start(f32[128,512]{1,0:T(8,128)S(1)} %get-tuple-element.26), channel_id=1, source_target_pairs={{0,2},{2,0},{1,3},{3,1},{4,6},{6,4},{5,7},{7,5},{8,10},{10,8},{9,1... | collective-permute-start | bytes 786440 | tf_op jit(solution)/shard_map/ppermute | solution.py:333
  88.4 10.2 %collective-permute-start.18 = (bf16[3,128,384]{2,1,0:T(8,128)(2,1)}, bf16[3,128,384]{2,1,0:T(8,128)(2,1)S(1)}, u32[]{:S(2)}, u32[]{:S(2)}) collective-permute-start(bf16[3,128,384]{2,1,0:T(8,128)(2,1)} %collective-permute-done.14.refs_3_), channel_id=1, source_target_pairs={{0,1},{1,0},{2,3},{3,2},{4,5},{5,4},{6,7},{7,6},{8,9},{9,8},{10,11... | collective-permute-start | bytes 884744 | tf_op jit(solution)/shard_map/ppermute | solution.py:333
  88.4 6.0 %collective-permute-start.7 = (bf16[128,512]{1,0:T(8,128)(2,1)S(1)}, bf16[128,512]{1,0:T(8,128)(2,1)S(1)}, u32[]{:S(2)}, u32[]{:S(2)}) collective-permute-start(bf16[128,512]{1,0:T(8,128)(2,1)S(1)} %add_convert_fusion.here), channel_id=1, source_target_pairs={{0,2},{2,0},{1,3},{3,1},{4,6},{6,4},{5,7},{7,5},{8,10},{10,8},{9,1... | collective-permute-start | bytes 393224 | tf_op jit(solution)/shard_map/ppermute | solution.py:333
  90.0 18.5 %collective-permute-start.8 = (bf16[128,512]{1,0:T(8,128)(2,1)S(1)}, bf16[128,512]{1,0:T(8,128)(2,1)S(1)}, u32[]{:S(2)}, u32[]{:S(2)}) collective-permute-start(bf16[128,512]{1,0:T(8,128)(2,1)S(1)} %add_convert_fusion.here), channel_id=1, source_target_pairs={{0,1},{1,0},{2,3},{3,2},{4,5},{5,4},{6,7},{7,6},{8,9},{9,8},{10,11... | collective-permute-start | bytes 393224 | tf_op jit(solution)/shard_map/ppermute | solution.py:333
  94.4 15.6 %collective-permute-start.9 = (bf16[128,512]{1,0:T(8,128)(2,1)S(1)}, bf16[128,512]{1,0:T(8,128)(2,1)S(1)}, u32[]{:S(2)}, u32[]{:S(2)}) collective-permute-start(bf16[128,512]{1,0:T(8,128)(2,1)S(1)} %collective-permute-done.7.there), channel_id=1, source_target_pairs={{0,1},{1,0},{2,3},{3,2},{4,5},{5,4},{6,7},{7,6},{8,9},{9,8},{10,11... | collective-permute-start | bytes 393224 | tf_op jit(solution)/shard_map/ppermute | solution.py:333
  98.6 7.9 %collective-permute-start.29 = (bf16[128,256]{1,0:T(8,128)(2,1)S(1)}, bf16[128,256]{1,0:T(8,128)(2,1)S(1)}, u32[]{:S(2)}, u32[]{:S(2)}) collective-permute-start(bf16[128,256]{1,0:T(8,128)(2,1)S(1)} %get-tuple-element.40), channel_id=1, source_target_pairs={{0,4},{4,0},{8,12},{12,8},{1,5},{5,1},{9,13},{13,9},{2,6},{6,2},{1... | collective-permute-start | bytes 196616 | tf_op jit(solution)/shard_map/ppermute | solution.py:337
  106.5 13.9 %collective-permute-start.30 = (bf16[128,256]{1,0:T(8,128)(2,1)S(1)}, bf16[128,256]{1,0:T(8,128)(2,1)S(1)}, u32[]{:S(2)}, u32[]{:S(2)}) collective-permute-start(bf16[128,256]{1,0:T(8,128)(2,1)S(1)} %get-tuple-element.41), channel_id=1, source_target_pairs={{0,8},{4,12},{8,0},{12,4},{1,9},{5,13},{9,1},{13,5},{2,10},{6,14},... | collective-permute-start | bytes 196616 | tf_op jit(solution)/shard_map/ppermute | solution.py:337
  108.5 12.0 %collective-permute-start.31 = (bf16[128,256]{1,0:T(8,128)(2,1)S(1)}, bf16[128,256]{1,0:T(8,128)(2,1)S(1)}, u32[]{:S(2)}, u32[]{:S(2)}) collective-permute-start(bf16[128,256]{1,0:T(8,128)(2,1)S(1)} %get-tuple-element.42), channel_id=1, source_target_pairs={{0,12},{4,8},{8,4},{12,0},{1,13},{5,9},{9,5},{13,1},{2,14},{6,10},... | collective-permute-start | bytes 196616 | tf_op jit(solution)/shard_map/ppermute | solution.py:337
  110.0 10.5 %collective-permute-start.19 = (bf16[128,384]{1,0:T(8,128)(2,1)S(1)}, bf16[128,384]{1,0:T(8,128)(2,1)S(1)}, u32[]{:S(2)}, u32[]{:S(2)}) collective-permute-start(bf16[128,384]{1,0:T(8,128)(2,1)S(1)} %get-tuple-element.32), channel_id=1, source_target_pairs={{0,4},{4,0},{8,12},{12,8},{1,5},{5,1},{9,13},{13,9},{2,6},{6,2},{1... | collective-permute-start | bytes 294920 | tf_op jit(solution)/shard_map/ppermute | solution.py:337
  110.6 12.3 %collective-permute-start.20 = (bf16[128,384]{1,0:T(8,128)(2,1)S(1)}, bf16[128,384]{1,0:T(8,128)(2,1)S(1)}, u32[]{:S(2)}, u32[]{:S(2)}) collective-permute-start(bf16[128,384]{1,0:T(8,128)(2,1)S(1)} %get-tuple-element.33), channel_id=1, source_target_pairs={{0,8},{4,12},{8,0},{12,4},{1,9},{5,13},{9,1},{13,5},{2,10},{6,14},... | collective-permute-start | bytes 294920 | tf_op jit(solution)/shard_map/ppermute | solution.py:337
  112.9 10.0 %collective-permute-start.21 = (bf16[128,384]{1,0:T(8,128)(2,1)S(1)}, bf16[128,384]{1,0:T(8,128)(2,1)S(1)}, u32[]{:S(2)}, u32[]{:S(2)}) collective-permute-start(bf16[128,384]{1,0:T(8,128)(2,1)S(1)} %get-tuple-element.34), channel_id=1, source_target_pairs={{0,12},{4,8},{8,4},{12,0},{1,13},{5,9},{9,5},{13,1},{2,14},{6,10},... | collective-permute-start | bytes 294920 | tf_op jit(solution)/shard_map/ppermute | solution.py:337
  (22 other events, 261.2 us)
